TPU v7x, 256 devices: a whole 4x4x8 slice. The times are simulated.
256 devices in a mesh: dp: 8 (over y, core), tensor: 4 (over x), ctx: 8 (over z).
Axes of the slice: x: 4, y: 4, z: 8, core: 2. Of those that a mesh axis runs over, the one named last changes fastest.
Arguments:
- grad_down: bfloat16 [8, 18432, 4608], P('dp', 'tensor', 'ctx'), may hold values from -700 to 700
- grad_query: bfloat16 [8, 4608, 2048], P('dp', 'ctx', 'tensor'), may hold values from -700 to 700
- down_param: float32 [18432, 4608], P(('tensor', 'dp'), 'ctx'), may hold values from -0.3 to 0.3
- down_moment: float32 [18432, 4608], P(('tensor', 'dp'), 'ctx'), may hold values from -6 to 6
- down_second: float32 [4608], P('ctx'), may hold values from 0.1 to 2
- query_param: float32 [4608, 2048], P(('ctx', 'dp'), 'tensor'), may hold values from -0.3 to 0.3
- query_moment: float32 [4608, 2048], P(('ctx', 'dp'), 'tensor'), may hold values from -6 to 6
- query_second: float32 [16], P('tensor'), may hold values from 0.1 to 2
- step_count: int32 [1], replicated, may hold values from 1 to 29
Outputs:
- down_param_new: float32 [18432, 4608], P(('tensor', 'dp'), 'ctx')
- down_moment_new: float32 [18432, 4608], P(('tensor', 'dp'), 'ctx')
- down_second_new: float32 [4608], P('ctx')
- down_update: bfloat16 [18432, 4608], P(('tensor', 'dp'), 'ctx')
- query_param_new: float32 [4608, 2048], P(('ctx', 'dp'), 'tensor')
- query_moment_new: float32 [4608, 2048], P(('ctx', 'dp'), 'tensor')
- query_second_new: float32 [16], P('tensor')
- query_update: bfloat16 [4608, 2048], P(('ctx', 'dp'), 'tensor')
All inputs are finite; a program needn't handle non-finite values.
Results may differ from a plain program's by a relative error of at most 0.012.
Values may be sent and summed in bfloat16 or wider, within the bound.
A program may use at most 64 MiB of HBM per device.

v0:
```python
import jax
import jax.numpy as jnp
from jax import lax
from jax.sharding import PartitionSpec as P

D = 4608
HEAD_DIM = 128
FF = 18432


BETA_ONE = 0.9
BETA_TWO = 0.95
EPSILON = 1e-08
LEARN_RATE = 0.003
DECAY_RATE = 0.1


def sent_to_all(shard, axis):
    copies = jnp.broadcast_to(shard, (lax.axis_size(axis), *shard.shape))
    return lax.all_to_all(copies, axis, split_axis=0, concat_axis=0, tiled=True)


def over_copies(shard, axis):
    everything = sent_to_all(shard, axis)
    return jnp.sum(everything, axis=0)


def finish(parameter, moment, gradient, second_wide, keep_one, keep_two):
    moment_new = BETA_ONE * moment + (1.0 - BETA_ONE) * gradient
    update = moment_new / keep_one / (jnp.sqrt(second_wide / keep_two) + EPSILON)
    parameter_new = parameter - LEARN_RATE * (update + DECAY_RATE * parameter)
    return (parameter_new, moment_new, update.astype(jnp.bfloat16))


def shards(
    grad_down,
    grad_query,
    down_param,
    down_moment,
    down_second,
    query_param,
    query_moment,
    query_second,
    step_count,
):
    replicas = lax.axis_size("dp")
    step_value = step_count[0].astype(jnp.float32)
    keep_one = 1.0 - jnp.power(jnp.float32(BETA_ONE), step_value)
    keep_two = 1.0 - jnp.power(jnp.float32(BETA_TWO), step_value)
    down_summed, query_summed = (
        lax.psum_scatter(grad_down[0], "dp", scatter_dimension=0, tiled=True).astype(jnp.float32),
        lax.psum_scatter(grad_query[0], "dp", scatter_dimension=0, tiled=True).astype(jnp.float32),
    )
    down_grad = down_summed / replicas
    neuron_part = jnp.sum(down_grad * down_grad, axis=0)
    query_grad = query_summed / replicas
    head_count = query_grad.shape[1] // HEAD_DIM
    head_part = jnp.sum(
        (query_grad * query_grad).reshape(query_grad.shape[0], head_count, HEAD_DIM), axis=(0, 2)
    )
    neuron_total = over_copies(neuron_part, ("dp", "tensor"))
    head_total = over_copies(head_part, ("dp", "ctx"))
    down_second_new = BETA_TWO * down_second + (1.0 - BETA_TWO) * (neuron_total / FF)
    query_second_new = BETA_TWO * query_second + (1.0 - BETA_TWO) * (head_total / (D * HEAD_DIM))
    down_param_new, down_moment_new, down_update = finish(
        down_param, down_moment, down_grad, down_second_new[None, :], keep_one, keep_two
    )
    query_wide = jnp.repeat(query_second_new, HEAD_DIM)
    query_param_new, query_moment_new, query_update = finish(
        query_param, query_moment, query_grad, query_wide[None, :], keep_one, keep_two
    )
    return (
        down_param_new,
        down_moment_new,
        down_second_new,
        down_update,
        query_param_new,
        query_moment_new,
        query_second_new,
        query_update,
    )


def solution(mesh):
    in_specs = (
        P("dp", "tensor", "ctx"),
        P("dp", "ctx", "tensor"),
        P(("tensor", "dp"), "ctx"),
        P(("tensor", "dp"), "ctx"),
        P("ctx"),
        P(("ctx", "dp"), "tensor"),
        P(("ctx", "dp"), "tensor"),
        P("tensor"),
        P(),
    )
    out_specs = (
        P(("tensor", "dp"), "ctx"),
        P(("tensor", "dp"), "ctx"),
        P("ctx"),
        P(("tensor", "dp"), "ctx"),
        P(("ctx", "dp"), "tensor"),
        P(("ctx", "dp"), "tensor"),
        P("tensor"),
        P(("ctx", "dp"), "tensor"),
    )
    return jax.shard_map(shards, mesh=mesh, in_specs=in_specs, out_specs=out_specs, check_vma=False)
```

profile of v0, /device:TPU:1, one launch (start us, length us, event | category | flops | bytes accessed | tf_op | source)
XLA Modules:
  0.0 119.7 jit_solution(1090725147647718968)
XLA Ops:
  7.2 0.7 reduce-scatter.5.cloned.1.call-update
  7.9 0.0 reduce-scatter.3.cloned.1.call-start
  7.9 8.4 %copy.19 = bf16[1,4608,576]{2,1,0:T(8,128)(2,1)} copy(bf16[1,4608,576]{1,2,0:T(8,128)(2,1)} %param.9) | data formatting | bytes 10616832 | tf_op args[0]
  16.4 29.7 %reduce-scatter.5.cloned.1.call-done = bf16[72,512]{1,0:T(8,128)(2,1)} async-done(((bf16[576,512]{1,0:T(8,128)(2,1)}), bf16[72,512]{1,0:T(8,128)(2,1)}) %reduce-scatter.5.cloned.1.call-update) | async-done | bytes 73744 | tf_op jit(solution)/shard_map/reduce_scatter | solution.py:52
  46.1 0.9 fusion.6
  47.0 0.1 bitcast_reduce_fusion
  47.1 0.6 broadcast_in_dim.11
  47.8 10.5 %all-to-all-start.1 = ((f32[64,1,4]{2,1,0:T(1,128)}), f32[64,1,4]{2,1,0:T(1,128)S(1)}, u32[]{:S(2)}, u32[]{:S(2)}) async-start(f32[64,1,4]{2,1,0:T(1,128)} %broadcast_in_dim.11), calls=%async_computation.3 | async-start | bytes 65536 | tf_op jit(solution)/shard_map/all_to_all | solution.py:20
  59.0 8.4 %all-to-all-done.1 = f32[64,1,4]{2,1,0:T(1,128)S(1)} async-done(((f32[64,1,4]{2,1,0:T(1,128)}), f32[64,1,4]{2,1,0:T(1,128)S(1)}, u32[]{:S(2)}, u32[]{:S(2)}) %all-to-all-start.1) | async-done | bytes 1056 | tf_op jit(solution)/shard_map/all_to_all | solution.py:20
  67.4 0.1 reduce_sum.48
  67.5 0.5 add_multiply_fusion.1
  68.0 0.1 broadcast_bitcast_fusion
  68.1 1.5 %fusion.7 = (bf16[72,512]{1,0:T(8,128)(2,1)}, f32[72,512]{1,0:T(8,128)S(1)}) fusion(f32[512]{0:T(512)S(1)} %broadcast_bitcast_fusion, bf16[72,512]{1,0:T(8,128)(2,1)} %reduce-scatter.5.cloned.1.call-done, f32[72,512]{1,0:T(8,128)S(1)} %copy-done.5), kind=kLoop, calls=%fused_computation.15 | loop fusion | flops 221184 | bytes 444416 | tf_op jit(solution)/shard_map/convert_element_type | solution.py:32
  69.6 22.9 %reduce-scatter.3.cloned.1.call-done = bf16[576,576]{1,0:T(8,128)(2,1)} async-done(((bf16[4608,576]{1,0:T(8,128)(2,1)}), bf16[576,576]{1,0:T(8,128)(2,1)}) %reduce-scatter.3.cloned.1.call-update) | async-done | bytes 663568 | tf_op jit(solution)/shard_map/reduce_scatter | solution.py:51
  92.6 1.4 %fusion.2 = f32[576]{0:T(1024)S(1)} fusion(bf16[576,576]{1,0:T(8,128)(2,1)} %reduce-scatter.3.cloned.1.call-done), kind=kLoop, calls=%fused_computation.4 | loop fusion | flops 1326528 | bytes 665856 | tf_op jit(solution)/shard_map/reduce_sum | solution.py:55
  94.0 0.7 broadcast_in_dim.10
  94.6 7.2 %all-to-all-start = ((f32[32,1,576]{2,1,0:T(1,128)}), f32[32,1,576]{2,1,0:T(1,128)S(1)}, u32[]{:S(2)}, u32[]{:S(2)}) async-start(f32[32,1,576]{2,1,0:T(1,128)} %broadcast_in_dim.10), calls=%async_computation.1 | async-start | bytes 163840 | tf_op jit(solution)/shard_map/all_to_all | solution.py:20
  101.9 0.7 multiply_subtract_fusion.1
  102.6 6.6 %all-to-all-done = f32[32,1,576]{2,1,0:T(1,128)S(1)} async-done(((f32[32,1,576]{2,1,0:T(1,128)}), f32[32,1,576]{2,1,0:T(1,128)S(1)}, u32[]{:S(2)}, u32[]{:S(2)}) %all-to-all-start) | async-done | bytes 73760 | tf_op jit(solution)/shard_map/all_to_all | solution.py:20
  109.1 0.1 reduce_sum.44
  109.2 0.6 add_multiply_fusion
  109.8 1.1 fusion.3
  111.0 0.5 copy-done.3
  111.5 1.4 %multiply_subtract_fusion = f32[576,576]{1,0:T(8,128)} fusion(f32[576,576]{1,0:T(8,128)S(1)} %copy-done.3, f32[576,576]{1,0:T(8,128)S(1)} %get-tuple-element.13, f32[576]{0:T(1024)S(1)} %get-tuple-element.14), kind=kLoop, calls=%fused_computation.5 | loop fusion | flops 1658880 | bytes 3983616 | tf_op jit(solution)/shard_map/sub | solution.py:31
  (19 shorter events, 0.1 us)
Async XLA Ops:
  7.2 38.9 %reduce-scatter.5.cloned.1.call-start = ((), (), s32[]{:S(2)}) async-start(), calls=%async_computation.5 | async-start | bytes 663552 | tf_op jit(solution)/shard_map/reduce_scatter | solution.py:52
  7.9 84.6 %reduce-scatter.3.cloned.1.call-start = ((), (), s32[]{:S(2)}) async-start(), calls=%async_computation.4 | async-start | bytes 6635520 | tf_op jit(solution)/shard_map/reduce_scatter | solution.py:51
  16.3 51.2 %copy-start.8 = (f32[4]{0:T(128)S(1)}, f32[4]{0:T(128)}, u32[]{:S(2)}) copy-start(f32[4]{0:T(128)} %param.16) | copy-start | bytes 52
  16.3 51.7 %copy-start.5 = (f32[72,512]{1,0:T(8,128)S(1)}, f32[72,512]{1,0:T(8,128)}, u32[]{:S(2)}) copy-start(f32[72,512]{1,0:T(8,128)} %param.15) | copy-start | bytes 442372
  16.3 85.5 %copy-start.6 = (f32[72,512]{1,0:T(8,128)S(1)}, f32[72,512]{1,0:T(8,128)}, u32[]{:S(2)}) copy-start(f32[72,512]{1,0:T(8,128)} %param.14) | copy-start | bytes 442372
  16.4 92.8 %copy-start.7 = (f32[576]{0:T(1024)S(1)}, f32[576]{0:T(1024)}, u32[]{:S(2)}) copy-start(f32[576]{0:T(1024)} %param.13) | copy-start | bytes 6916
  16.4 93.4 %copy-start.2 = (f32[576,576]{1,0:T(8,128)S(1)}, f32[576,576]{1,0:T(8,128)}, u32[]{:S(2)}) copy-start(f32[576,576]{1,0:T(8,128)} %param.12) | copy-start | bytes 3981316
  47.8 19.7 %all-to-all-start.1 = ((f32[64,1,4]{2,1,0:T(1,128)}), f32[64,1,4]{2,1,0:T(1,128)S(1)}, u32[]{:S(2)}, u32[]{:S(2)}) async-start(f32[64,1,4]{2,1,0:T(1,128)} %broadcast_in_dim.11), calls=%async_computation.3 | async-start | bytes 65536 | tf_op jit(solution)/shard_map/all_to_all | solution.py:20
  69.6 41.3 %copy-start.4 = (f32[72,512]{1,0:T(8,128)}, f32[72,512]{1,0:T(8,128)S(1)}, u32[]{:S(2)}) copy-start(f32[72,512]{1,0:T(8,128)S(1)} %get-tuple-element.9) | copy-start | bytes 442372
  92.5 17.3 %copy-start.1 = (bf16[576,576]{1,0:T(8,128)(2,1)S(1)}, bf16[576,576]{1,0:T(8,128)(2,1)}, u32[]{:S(2)}) copy-start(bf16[576,576]{1,0:T(8,128)(2,1)} %reduce-scatter.3.cloned.1.call-done) | copy-start | bytes 1990660
  94.6 14.5 %all-to-all-start = ((f32[32,1,576]{2,1,0:T(1,128)}), f32[32,1,576]{2,1,0:T(1,128)S(1)}, u32[]{:S(2)}, u32[]{:S(2)}) async-start(f32[32,1,576]{2,1,0:T(1,128)} %broadcast_in_dim.10), calls=%async_computation.1 | async-start | bytes 163840 | tf_op jit(solution)/shard_map/all_to_all | solution.py:20
  109.8 1.6 %copy-start.3 = (f32[576,576]{1,0:T(8,128)S(1)}, f32[576,576]{1,0:T(8,128)}, u32[]{:S(2)}) copy-start(f32[576,576]{1,0:T(8,128)} %param.11) | copy-start | bytes 3981316
  111.0 1.9 %copy-start = (f32[576,576]{1,0:T(8,128)}, f32[576,576]{1,0:T(8,128)S(1)}, u32[]{:S(2)}) copy-start(f32[576,576]{1,0:T(8,128)S(1)} %get-tuple-element.13) | copy-start | bytes 3981316
Sparse Core Ops, SparseCore 0:
  10.5 35.5 reduce-scatter.4
  48.6 43.8 reduce-scatter.2
where the time goes:
time: 120 us
  waiting for transfers between devices  68.3 us (57%)
  starting transfers between devices  17.8 us (15%)
  between operations  14.8 us (12%)
  local copies, waits for them, and re-layouts  10.3 us (9%)
  other arithmetic  8.47 us (7%)
    reduce_scatter x1, waiting for transfers between devices, shards(): lax.psum_scatter(grad_query[0], 'dp', scatter_dimension=0, tiled=True)  29.7 us
    reduce_scatter x1, waiting for transfers between devices, shards(): lax.psum_scatter(grad_down[0], 'dp', scatter_dimension=0, tiled=True)  22.9 us
    all_to_all x2, starting transfers between devices, sent_to_all(): return lax.all_to_all(copies, axis, split_axis=0, concat_axis=0, tiled=True)  17.7 us
    all_to_all x2, waiting for transfers between devices, sent_to_all(): return lax.all_to_all(copies, axis, split_axis=0, concat_axis=0, tiled=True)  15 us
    unnamed x19, local copies, waits for them, and re-layouts  8.92 us
    convert_element_type x2, other arithmetic, finish(): return (parameter_new, moment_new, update.astype(jnp.bfloat16))  2.69 us
  transfers between devices with their start and end apart: 4, of which 4 were waited for; matrix products, arithmetic and copies ran while one was open for 11% of the time, Pallas kernels for 0%

commit v1 on v0

v1 whole, which is shorter than its diff:
```python
import functools
import math

import jax
import jax.numpy as jnp
from jax import lax
from jax.experimental import pallas as pl
from jax.experimental.pallas import tpu as pltpu
from jax.sharding import PartitionSpec as P

D = 4608
HEAD_DIM = 128
FF = 18432

BETA_ONE = 0.9
BETA_TWO = 0.95
EPSILON = 1e-08
LEARN_RATE = 0.003
DECAY_RATE = 0.1

MESH = pl.DeviceIdType.MESH
F32 = jnp.float32
BF16 = jnp.bfloat16

FAR, RIGHT, LEFT, SELF = range(4)
PLUS, MINUS = range(2)
LANES = 128
TILES = 4


def exchange(
    gd, gq, steps, dsec, qsec,
    g_out, t_out, q_out, n_out,
    own_d, prt_d, own_t, prt_t, own_q, prt_q,
    snd_a, snd_b, snd_t, snd_q, rly_a, rly_b, rly_t, rly_q,
    fin_pa, fin_pb, fin_ma, fin_mb, fin_tp, fin_tm, fin_q,
    tbuf, zbuf, dbuf, xbuf, dsec_v, qsec_v,
    own_sem, ds_sem, dr_sem, ss, rs_rly, rs_fin, tsem, zs, zr, ps, pr, xs, xr, small_sem,
):
    dp, tp, cp = lax.axis_index("dp"), lax.axis_index("tensor"), lax.axis_index("ctx")
    y, core = dp // 2, dp % 2
    nz = zbuf.shape[0]
    cols_all, wide = own_d.shape[1], own_d.shape[2]
    cut = 2 * LANES
    rest = cols_all - cut
    t_cols = cols_all // 2
    pair = 2 * wide + LANES
    rows_q, q_cols = own_q.shape[1], own_q.shape[2]
    q_half = q_cols // 2
    at = {FAR: (y + 2) % 4, RIGHT: (y + 1) % 4, LEFT: (y + 3) % 4, SELF: y}
    partner = y * 2 + (1 - core)

    span = {"A": (0, cut), "B": (cut, rest), "AB": (0, cols_all)}

    def main_piece(role, who, part, first, tiles):
        row, count = span[part]
        lanes = pl.multiple_of(at[role] * pair + who * (wide + LANES) + first * LANES, LANES)
        return gd.at[0, pl.ds(row, count), pl.ds(lanes, tiles * LANES)]

    def tile_piece(role, who):
        lanes = pl.multiple_of(at[role] * pair + wide, LANES)
        return gd.at[0, pl.ds(pl.multiple_of(who * t_cols, 16), t_cols), pl.ds(lanes, LANES)]

    def query_piece(role, who):
        return gq.at[0, pl.ds(pl.multiple_of((at[role] * 2 + who) * rows_q, 8), rows_q), :]

    order = [("q", FAR), ("t", FAR)] + [("d", FAR, "AB", k, 1) for k in range(TILES)]
    order += [("q", RIGHT), ("q", LEFT), ("d", RIGHT, "B", 0, TILES), ("t", LEFT), ("d", LEFT, "A", 0, TILES)]
    order += [("t", RIGHT), ("d", RIGHT, "A", 0, TILES), ("d", LEFT, "B", 0, TILES)]
    order += [("q", SELF), ("t", SELF), ("d", SELF, "AB", 0, TILES)]

    def piece(item, who):
        if item[0] == "q":
            return query_piece(item[1], who)
        if item[0] == "t":
            return tile_piece(item[1], who)
        return main_piece(item[1], who, *item[2:])

    def landing(item, d, t, q):
        if item[0] == "q":
            return q.at[item[1]]
        if item[0] == "t":
            return t.at[item[1]]
        _, role, part, first, tiles = item
        row, count = span[part]
        return d.at[role, pl.ds(row, count), pl.ds(first * LANES, tiles * LANES)]

    own_copy = [
        pltpu.make_async_copy(piece(item, core), landing(item, own_d, own_t, own_q), own_sem.at[n])
        for n, item in enumerate(order)
    ]
    for copy in own_copy:
        copy.start()

    barrier = pltpu.get_barrier_semaphore()
    greeted = 0
    for k in range(1, 8):
        pl.semaphore_signal(barrier, inc=1, device_id=((dp + k) % 8, tp, cp), device_id_type=MESH)
        greeted += 1
    for k in range(1, 4):
        pl.semaphore_signal(barrier, inc=1, device_id=(dp, (tp + k) % 4, cp), device_id_type=MESH)
        greeted += 1
    for k in (1, nz - 1):
        pl.semaphore_signal(barrier, inc=1, device_id=(dp, tp, (cp + k) % nz), device_id_type=MESH)
        greeted += 1
    pl.semaphore_wait(barrier, greeted)

    prt_copy = [
        pltpu.make_async_remote_copy(
            src_ref=piece(item, 1 - core), dst_ref=landing(item, prt_d, prt_t, prt_q),
            send_sem=ds_sem.at[n], recv_sem=dr_sem.at[n],
            device_id=(partner, tp, cp), device_id_type=MESH)
        for n, item in enumerate(order)
    ]
    for copy in prt_copy:
        copy.start()

    small = [
        pltpu.make_async_copy(dsec, dsec_v, small_sem.at[1]),
        pltpu.make_async_copy(qsec, qsec_v, small_sem.at[2]),
    ]
    for copy in small:
        copy.start()

    have = set()

    def need(test):
        for n, item in enumerate(order):
            if n not in have and test(item):
                have.add(n)
                own_copy[n].wait()
                prt_copy[n].wait_recv()

    def main_sum(role, part, k):
        need(lambda item: item[0] == "d" and item[1] == role and part in item[2] and item[3] <= k < item[3] + item[4])
        row, count = span[part]
        here = (role, pl.ds(row, count), pl.ds(k * LANES, LANES))
        return own_d[here].astype(F32) + prt_d[here].astype(F32)

    def tile_sum(role):
        need(lambda item: item == ("t", role))
        return own_t[role].astype(F32) + prt_t[role].astype(F32)

    def query_sum(role, block):
        need(lambda item: item == ("q", role))
        here = (role, slice(None), pl.ds(block * q_half, q_half))
        return own_q[here].astype(F32) + prt_q[here].astype(F32)

    y_copies = []
    counters = {"s": 0, "r": 0, "f": 0}

    def y_send(direction, src, dst, landing_sems, kind):
        target = at[RIGHT] if direction == PLUS else at[LEFT]
        s, r = counters["s"], counters[kind]
        counters["s"] += 1
        counters[kind] += 1
        copy = pltpu.make_async_remote_copy(
            src_ref=src, dst_ref=dst, send_sem=ss.at[s], recv_sem=landing_sems.at[r],
            device_id=(target * 2 + core, tp, cp), device_id_type=MESH)
        copy.start()
        y_copies.append(copy)
        return copy

    relayed, plain, joined = {}, {}, {}

    def store_send(direction, value, src, dst, landing_sems, kind):
        src[...] = value.astype(BF16)
        return y_send(direction, src, dst, landing_sems, kind)

    def first_q():
        for way in (PLUS, MINUS):
            relayed[way, "q"] = store_send(way, query_sum(FAR, way), snd_q.at[way, 0], rly_q.at[way], rs_rly, "r")

    def second_q():
        for way, role in ((PLUS, RIGHT), (MINUS, LEFT)):
            plain[way, "q"] = store_send(way, query_sum(role, 1 - way), snd_q.at[way, 1], fin_q.at[way, 0], rs_fin, "f")

    def third_q():
        for way, role in ((PLUS, RIGHT), (MINUS, LEFT)):
            relayed[way, "q"].wait_recv()
            value = query_sum(role, way) + rly_q[way].astype(F32)
            joined[way, "q"] = store_send(way, value, snd_q.at[way, 2], fin_q.at[way, 1], rs_fin, "f")

    def first_t():
        relayed["t"] = store_send(PLUS, tile_sum(FAR), snd_t.at[0], rly_t, rs_rly, "r")

    def second_t():
        plain["t"] = store_send(MINUS, tile_sum(LEFT), snd_t.at[1], fin_tm, rs_fin, "f")

    def third_t():
        relayed["t"].wait_recv()
        value = tile_sum(RIGHT) + rly_t[...].astype(F32)
        joined["t"] = store_send(PLUS, value, snd_t.at[2], fin_tp, rs_fin, "f")

    def first_d(k):
        relayed[PLUS, k] = store_send(PLUS, main_sum(FAR, "A", k), snd_a.at[0, k], rly_a.at[k], rs_rly, "r")
        relayed[MINUS, k] = store_send(MINUS, main_sum(FAR, "B", k), snd_b.at[0, k], rly_b.at[k], rs_rly, "r")

    def second_d(k):
        plain[PLUS, k] = store_send(PLUS, main_sum(RIGHT, "B", k), snd_b.at[1, k], fin_pb.at[k], rs_fin, "f")
        plain[MINUS, k] = store_send(MINUS, main_sum(LEFT, "A", k), snd_a.at[1, k], fin_ma.at[k], rs_fin, "f")

    def third_d(k):
        relayed[PLUS, k].wait_recv()
        value = main_sum(RIGHT, "A", k) + rly_a[k].astype(F32)
        joined[PLUS, k] = store_send(PLUS, value, snd_a.at[2, k], fin_pa.at[k], rs_fin, "f")
        relayed[MINUS, k].wait_recv()
        value = main_sum(LEFT, "B", k) + rly_b[k].astype(F32)
        joined[MINUS, k] = store_send(MINUS, value, snd_b.at[2, k], fin_mb.at[k], rs_fin, "f")

    first_q()
    first_t()
    first_d(0)
    second_q()
    first_d(1)
    third_q()
    first_d(2)
    first_d(3)
    second_t()
    for k in range(TILES):
        second_d(k)
    third_t()
    for k in range(TILES):
        third_d(k)

    head_row = jnp.zeros((1, LANES), F32)
    lane = lax.broadcasted_iota(jnp.int32, (1, LANES), 1)
    for block in (0, 1):
        joined[block, "q"].wait_recv()
        plain[1 - block, "q"].wait_recv()
        mean = (query_sum(SELF, block) + fin_q[block, 1].astype(F32) + fin_q[1 - block, 0].astype(F32)) / 8
        q_out[:, pl.ds(block * q_half, q_half)] = mean
        square = jnp.sum(mean * mean, axis=0, keepdims=True)
        for h in range(2):
            part = jnp.sum(square[:, h * LANES:(h + 1) * LANES], axis=1, keepdims=True)
            head_row = jnp.where(lane == block * 2 + h, part, head_row)
    zbuf[cp] = jnp.broadcast_to(head_row, (8, LANES))

    ring, z_copies = {}, []
    for s in range(nz // 2):
        for way, count in ((PLUS, nz // 2), (MINUS, nz - 1 - nz // 2)):
            if s < count:
                if s > 0:
                    ring[way, s - 1].wait_recv()
                owner = (cp + (nz - s if way == PLUS else s)) % nz
                ring[way, s] = pltpu.make_async_remote_copy(
                    src_ref=zbuf.at[owner], dst_ref=zbuf.at[owner],
                    send_sem=zs.at[way, s], recv_sem=zr.at[way, s],
                    device_id=(dp, tp, (cp + (1 if way == PLUS else nz - 1)) % nz), device_id_type=MESH)
                ring[way, s].start()
                z_copies.append(ring[way, s])
    ring[PLUS, nz // 2 - 1].wait_recv()
    ring[MINUS, nz - 2 - nz // 2].wait_recv()
    head_sum = zbuf[0, pl.ds(0, 1), :]
    for z in range(1, nz):
        head_sum = head_sum + zbuf[z, pl.ds(0, 1), :]

    joined["t"].wait_recv()
    plain["t"].wait_recv()
    mine = pl.ds(pl.multiple_of(core * t_cols, 8), t_cols)
    tbuf[mine, :] = (tile_sum(SELF) + fin_tp[...].astype(F32) + fin_tm[...].astype(F32)) / 8
    swap = pltpu.make_async_remote_copy(
        src_ref=tbuf.at[mine, :], dst_ref=tbuf.at[mine, :], send_sem=tsem.at[0], recv_sem=tsem.at[1],
        device_id=(partner, tp, cp), device_id_type=MESH)
    swap.start()

    def column_squares(rows):
        return jnp.sum(rows * rows, axis=0, keepdims=True)

    sums_a, sums_b = jnp.zeros((1, cut), F32), jnp.zeros((1, rest), F32)
    for k in range(TILES):
        if k == 1:
            swap.wait_recv()
            both = jnp.transpose(tbuf[...])
            own_rows = jnp.where(core == 0, both[:LANES // 2], both[LANES // 2:])
            t_out[...] = own_rows
            sums_a = sums_a + column_squares(own_rows[:, :cut])
            sums_b = sums_b + column_squares(own_rows[:, cut:])
        plain[MINUS, k].wait_recv()
        joined[PLUS, k].wait_recv()
        mean = (main_sum(SELF, "A", k) + fin_pa[k].astype(F32) + fin_ma[k].astype(F32)) / 8
        rows = jnp.transpose(mean)
        g_out[k, :, pl.ds(0, cut)] = rows
        sums_a = sums_a + column_squares(rows)
        plain[PLUS, k].wait_recv()
        joined[MINUS, k].wait_recv()
        mean = (main_sum(SELF, "B", k) + fin_mb[k].astype(F32) + fin_pb[k].astype(F32)) / 8
        rows = jnp.transpose(mean)
        g_out[k, :, pl.ds(cut, rest)] = rows
        sums_b = sums_b + column_squares(rows)

    dbuf[dp] = jnp.zeros((8, LANES), F32)
    dbuf[dp, pl.ds(0, 1), :] = sums_a[:, :LANES]
    dbuf[dp, pl.ds(1, 1), :] = sums_a[:, LANES:]
    dbuf[dp, pl.ds(2, 1), :] = sums_b[:, :LANES]
    dbuf[dp, pl.ds(3, 1), :] = sums_b[:, LANES:2 * LANES]
    dbuf[dp, pl.ds(4, 1), pl.ds(0, LANES // 2)] = sums_b[:, 2 * LANES:]
    dbuf[dp, pl.ds(5, 1), :] = head_sum

    def to_all(buf, me, size, device, send, recv):
        sends = []
        for k in range(1, size):
            copy = pltpu.make_async_remote_copy(
                src_ref=buf.at[me], dst_ref=buf.at[me], send_sem=send.at[k], recv_sem=recv.at[me],
                device_id=device((me + k) % size), device_id_type=MESH)
            copy.start()
            sends.append(copy)
        for k in range(1, size):
            other = (me + k) % size
            pltpu.make_async_remote_copy(
                src_ref=buf.at[other], dst_ref=buf.at[other], send_sem=send.at[k], recv_sem=recv.at[other],
                device_id=device(other), device_id_type=MESH).wait_recv()
        total = buf[0]
        for p in range(1, size):
            total = total + buf[p]
        return total, sends

    for copy in small:
        copy.wait()
    step = jnp.full((1, LANES), steps[0], jnp.int32).astype(F32)
    keep_one = 1.0 - jnp.exp(step * math.log(BETA_ONE))
    keep_two = 1.0 - jnp.exp(step * math.log(BETA_TWO))

    part, p_copies = to_all(dbuf, dp, 8, lambda p: (p, tp, cp), ps, pr)
    xbuf[tp] = part
    whole, x_copies = to_all(xbuf, tp, 4, lambda t: (dp, t, cp), xs, xr)

    def advance(old, mean, n):
        new = BETA_TWO * old + (1.0 - BETA_TWO) * mean
        n_out[n:n + 1, :] = 1.0 / (keep_one * (jnp.sqrt(new / keep_two) + EPSILON))
        n_out[n + 8:n + 9, :] = new

    n_out[...] = jnp.zeros(n_out.shape, F32)
    for k in range(5):
        if k < 4:
            old = dsec_v[pl.ds(k * LANES, LANES)].reshape(1, LANES)
        else:
            old = dsec_v[pl.ds(k * LANES, LANES // 2)].reshape(1, LANES // 2)
            old = jnp.concatenate([old, jnp.ones((1, LANES // 2), F32)], axis=1)
        advance(old, whole[k:k + 1, :] / FF, k)
    old = jnp.ones((1, LANES), F32)
    for h in range(4):
        old = jnp.where(lane == h, qsec_v[h], old)
    advance(old, part[5:6, :] / (D * HEAD_DIM), 5)

    for copy in prt_copy + y_copies + z_copies + [swap] + p_copies + x_copies:
        copy.wait_send()


def finish(
    n_in, g_in, t_in, q_in, dp_in, dm_in, qp_in, qm_in,
    dp_out, dm_out, ds_out, du_out, qp_out, qm_out, qs_out, qu_out,
    po_buf, mo_buf, uo_buf, qpo, qmo, quo, out_sem,
):
    core = lax.axis_index("dp") % 2
    width = dp_in.shape[1]
    half = LANES // 2
    stores = []

    def store(src, dst):
        copy = pltpu.make_async_copy(src, dst, out_sem.at[len(stores)])
        copy.start()
        stores.append(copy)

    def update(param, moment, grad, scale):
        moment_new = BETA_ONE * moment + (1.0 - BETA_ONE) * grad
        step = moment_new * scale
        param_new = param - LEARN_RATE * (step + DECAY_RATE * param)
        return param_new, moment_new, step.astype(BF16)

    def down(grad, first, count):
        rows = pl.ds(pl.multiple_of(first, half), count)
        for k in range(5):
            lanes = pl.ds(k * LANES, LANES if k < 4 else width - 4 * LANES)
            scale = n_in[k:k + 1, :lanes.size]
            po_buf[rows, lanes], mo_buf[rows, lanes], uo_buf[rows, lanes] = update(
                dp_in[rows, lanes], dm_in[rows, lanes], grad[:, lanes], scale)
        store(po_buf.at[rows, :], dp_out.at[rows, :])
        store(mo_buf.at[rows, :], dm_out.at[rows, :])
        store(uo_buf.at[rows, :], du_out.at[rows, :])

    for k in range(TILES):
        down(g_in.at[k], core * half + k * LANES, LANES)
    down(t_in, (1 - core) * TILES * LANES, half)
    for h in range(4):
        lanes = pl.ds(h * LANES, LANES)
        qpo[:, lanes], qmo[:, lanes], quo[:, lanes] = update(
            qp_in[:, lanes], qm_in[:, lanes], q_in[:, lanes], n_in[5:6, h:h + 1])
    store(qpo, qp_out)
    store(qmo, qm_out)
    store(quo, qu_out)
    for k in range(5):
        count = LANES if k < 4 else width - 4 * LANES
        ds_out[pl.ds(k * LANES, count)] = n_in[8 + k:9 + k, :count].reshape(count)
    qs_out[...] = n_in[13:14, :4].reshape(4)
    for copy in stores:
        copy.wait()


def shards(nz, grad_down, grad_query, down_param, down_moment, down_second,
           query_param, query_moment, query_second, step_count):
    rows_d, width = down_param.shape
    rows_q, q_width = query_param.shape
    cut, wide = 2 * LANES, TILES * LANES
    rest, t_cols, q_half = width - cut, width // 2, q_width // 2
    hbm = pl.BlockSpec(memory_space=pltpu.HBM)
    vmem = pl.BlockSpec(memory_space=pltpu.VMEM)
    dma = pltpu.SemaphoreType.DMA
    pieces = 17
    grad_rows = jnp.swapaxes(grad_down, 1, 2)
    in_hbm = lambda x: pltpu.with_memory_space_constraint(x, pltpu.HBM)
    g, t, q, n = pl.pallas_call(
        exchange,
        name="exchange",
        out_shape=(
            jax.ShapeDtypeStruct((TILES, LANES, width), F32),
            jax.ShapeDtypeStruct((LANES // 2, width), F32),
            jax.ShapeDtypeStruct((rows_q, q_width), F32),
            jax.ShapeDtypeStruct((16, LANES), F32),
        ),
        in_specs=[hbm, hbm, pl.BlockSpec(memory_space=pltpu.SMEM), hbm, hbm],
        out_specs=(vmem,) * 4,
        scratch_shapes=[
            pltpu.VMEM((4, width, wide), BF16),
            pltpu.VMEM((4, width, wide), BF16),
            pltpu.VMEM((4, t_cols, LANES), BF16),
            pltpu.VMEM((4, t_cols, LANES), BF16),
            pltpu.VMEM((4, rows_q, q_width), BF16),
            pltpu.VMEM((4, rows_q, q_width), BF16),
            pltpu.VMEM((3, TILES, cut, LANES), BF16),
            pltpu.VMEM((3, TILES, rest, LANES), BF16),
            pltpu.VMEM((3, t_cols, LANES), BF16),
            pltpu.VMEM((2, 3, rows_q, q_half), BF16),
            pltpu.VMEM((TILES, cut, LANES), BF16),
            pltpu.VMEM((TILES, rest, LANES), BF16),
            pltpu.VMEM((t_cols, LANES), BF16),
            pltpu.VMEM((2, rows_q, q_half), BF16),
            pltpu.VMEM((TILES, cut, LANES), BF16),
            pltpu.VMEM((TILES, rest, LANES), BF16),
            pltpu.VMEM((TILES, cut, LANES), BF16),
            pltpu.VMEM((TILES, rest, LANES), BF16),
            pltpu.VMEM((t_cols, LANES), BF16),
            pltpu.VMEM((t_cols, LANES), BF16),
            pltpu.VMEM((2, 2, rows_q, q_half), BF16),
            pltpu.VMEM((width, LANES), F32),
            pltpu.VMEM((nz, 8, LANES), F32),
            pltpu.VMEM((8, 8, LANES), F32),
            pltpu.VMEM((4, 8, LANES), F32),
            pltpu.VMEM((width,), F32),
            pltpu.SMEM((4,), F32),
            dma((pieces,)), dma((pieces,)), dma((pieces,)),
            dma((33,)), dma((11,)), dma((22,)), dma((2,)),
            dma((2, nz)), dma((2, nz)), dma((8,)), dma((8,)), dma((4,)), dma((4,)), dma((3,)),
        ],
        compiler_params=pltpu.CompilerParams(
            collective_id=0, has_side_effects=True, vmem_limit_bytes=28 << 20),
    )(in_hbm(grad_rows), in_hbm(grad_query), step_count, in_hbm(down_second), in_hbm(query_second))

    return tuple(pl.pallas_call(
        finish,
        name="finish",
        out_shape=(
            jax.ShapeDtypeStruct((rows_d, width), F32),
            jax.ShapeDtypeStruct((rows_d, width), F32),
            jax.ShapeDtypeStruct((width,), F32),
            jax.ShapeDtypeStruct((rows_d, width), BF16),
            jax.ShapeDtypeStruct((rows_q, q_width), F32),
            jax.ShapeDtypeStruct((rows_q, q_width), F32),
            jax.ShapeDtypeStruct((4,), F32),
            jax.ShapeDtypeStruct((rows_q, q_width), BF16),
        ),
        in_specs=[vmem] * 8,
        out_specs=(hbm, hbm, vmem, hbm, hbm, hbm, vmem, hbm),
        scratch_shapes=[
            pltpu.VMEM((rows_d, width), F32),
            pltpu.VMEM((rows_d, width), F32),
            pltpu.VMEM((rows_d, width), BF16),
            pltpu.VMEM((rows_q, q_width), F32),
            pltpu.VMEM((rows_q, q_width), F32),
            pltpu.VMEM((rows_q, q_width), BF16),
            dma((3 * (TILES + 2),)),
        ],
        compiler_params=pltpu.CompilerParams(vmem_limit_bytes=24 << 20),
    )(n, g, t, q, down_param, down_moment, query_param, query_moment))


def solution(mesh):
    in_specs = (
        P("dp", "tensor", "ctx"),
        P("dp", "ctx", "tensor"),
        P(("tensor", "dp"), "ctx"),
        P(("tensor", "dp"), "ctx"),
        P("ctx"),
        P(("ctx", "dp"), "tensor"),
        P(("ctx", "dp"), "tensor"),
        P("tensor"),
        P(),
    )
    out_specs = (
        P(("tensor", "dp"), "ctx"),
        P(("tensor", "dp"), "ctx"),
        P("ctx"),
        P(("tensor", "dp"), "ctx"),
        P(("ctx", "dp"), "tensor"),
        P(("ctx", "dp"), "tensor"),
        P("tensor"),
        P(("ctx", "dp"), "tensor"),
    )
    body = functools.partial(shards, mesh.shape["ctx"])
    return jax.shard_map(body, mesh=mesh, in_specs=in_specs, out_specs=out_specs, check_vma=False)
```

time: 120 us -> 48.9 us (0.41)
  waiting for transfers between devices: 68.3 us -> 0 us
  Pallas kernels: 0 us -> 47.4 us
  starting transfers between devices: 17.8 us -> 0 us
  between operations: 14.8 us -> 1.35 us
  local copies, waits for them, and re-layouts: 10.3 us -> 0.02 us
  other arithmetic: 8.47 us -> 0 us
    reduce_scatter x2 -> x0, waiting for transfers between devices: 52.6 us -> none  [the longest x1 29.7 us: shards(): lax.psum_scatter(grad_query[0], 'dp', scatter_dimension=0, tiled=True)]
    pallas_call x0 -> x2, Pallas kernels: none -> 47.4 us  [the longest x1 44.6 us: shards(): pl.pallas_call(exchange, name='exchange', out_shape=(jax.ShapeDtypeStruct...]
    all_to_all x2 -> x0, starting transfers between devices: 17.7 us -> none  [sent_to_all(): return lax.all_to_all(copies, axis, split_axis=0, concat_axis=0, tiled=True)]
    all_to_all x2 -> x0, waiting for transfers between devices: 15 us -> none  [sent_to_all(): return lax.all_to_all(copies, axis, split_axis=0, concat_axis=0, tiled=True)]
    unnamed x19 -> x8, local copies, waits for them, and re-layouts: 8.92 us -> 0.02 us
    convert_element_type x2 -> x0, other arithmetic: 2.69 us -> none  [finish(): return (parameter_new, moment_new, update.astype(jnp.bfloat16))]
    reduce_sum x5 -> x0, other arithmetic: 2.6 us -> none  [the longest x1 1.42 us: shards(): neuron_part = jnp.sum(down_grad * down_grad, axis=0)]
    sub x2 -> x0, other arithmetic: 2.06 us -> none  [finish(): parameter_new = parameter - LEARN_RATE * (update + DECAY_RATE * parameter)]
  transfers between devices with their start and end apart: 4 -> 0, of which waited for: 4 -> 0; matrix products, arithmetic and copies ran while one was open for 11% -> 0% of each run, Pallas kernels for 0% -> 0%
where the time goes in v1:
time: 48.9 us; the launch traced here: 48.8 us
  Pallas kernels  47.4 us (97%)
  between operations  1.35 us (3%)
    pallas_call x1, Pallas kernels, shards(): pl.pallas_call(exchange, name='exchange', out_shape=(jax.ShapeDtypeStruct...  44.6 us
    pallas_call x1, Pallas kernels, shards(): pl.pallas_call(finish, name='finish', out_shape=(jax.ShapeDtypeStruct((ro...  2.85 us

profile of v1, /device:TPU:1, one launch (start us, length us, event | category | flops | bytes accessed | tf_op | source)
XLA Modules:
  0.0 48.8 jit_solution(3641510505718780917)
XLA Ops:
  1.3 0.0 copy-start
  1.3 0.0 copy-start.1
  1.3 0.0 copy-start.2
  1.3 0.0 copy-start.3
  1.3 44.6 %exchange.1 = (f32[4,128,576]{2,1,0:T(8,128)S(1)}, f32[64,576]{1,0:T(8,128)S(1)}, f32[72,512]{1,0:T(8,128)S(1)}, f32[16,128]{1,0:T(8,128)S(1)}) custom-call(bf16[1,576,4608]{2,1,0:T(8,128)(2,1)} %bitcast.1, bf16[1,576,512]{2,1,0:T(8,128)(2,1)} %gq.1, s32[1]{0:T(128)S(6)} %copy.17.steps, f32[576]{0:T(1024)} %dsec.1, f32[4]{0:T(128)} %qsec.1), custom_call_target="tpu_custom_call" | custom-call | tf_op jit(solution)/shard_map/exchange/pallas_call | solution.py:412
  45.9 0.0 copy-done
  45.9 0.0 copy-done.1
  45.9 0.0 copy-done.2
  45.9 0.0 copy-done.3
  45.9 2.9 %finish.1 = (f32[576,576]{1,0:T(8,128)}, f32[576,576]{1,0:T(8,128)}, f32[576]{0:T(1024)}, bf16[576,576]{1,0:T(8,128)(2,1)}, f32[72,512]{1,0:T(8,128)}, /*index=5...) custom-call(f32[16,128]{1,0:T(8,128)S(1)} %get-tuple-element.12.n_in, f32[4,128,576]{2,1,0:T(8,128)S(1)} %get-tuple-element.13.g_in, ...), custom_call_target="tpu_custom_call" | custom-call | tf_op jit(solution)/shard_map/finish/pallas_call | solution.py:459
Async XLA Ops:
  1.3 44.6 %copy-start = (f32[576,576]{1,0:T(8,128)S(1)}, f32[576,576]{1,0:T(8,128)}, u32[]{:S(2)}) copy-start(f32[576,576]{1,0:T(8,128)} %dp_in.1) | copy-start | bytes 3981316
  1.3 44.6 %copy-start.1 = (f32[576,576]{1,0:T(8,128)S(1)}, f32[576,576]{1,0:T(8,128)}, u32[]{:S(2)}) copy-start(f32[576,576]{1,0:T(8,128)} %dm_in.1) | copy-start | bytes 3981316
  1.3 44.6 %copy-start.2 = (f32[72,512]{1,0:T(8,128)S(1)}, f32[72,512]{1,0:T(8,128)}, u32[]{:S(2)}) copy-start(f32[72,512]{1,0:T(8,128)} %qp_in.1) | copy-start | bytes 442372
  1.3 44.6 %copy-start.3 = (f32[72,512]{1,0:T(8,128)S(1)}, f32[72,512]{1,0:T(8,128)}, u32[]{:S(2)}) copy-start(f32[72,512]{1,0:T(8,128)} %qm_in.1) | copy-start | bytes 442372

commit v2 on v1

--- a/solution.py
+++ b/solution.py
@@ -29,17 +29,17 @@
 
 
 def exchange(
-    gd, gq, steps, dsec, qsec,
-    g_out, t_out, q_out, n_out,
+    nz,
+    gd, gq, dm, qm, steps, dsec, qsec,
+    m_out, qm_out, n_out,
     own_d, prt_d, own_t, prt_t, own_q, prt_q,
     snd_a, snd_b, snd_t, snd_q, rly_a, rly_b, rly_t, rly_q,
     fin_pa, fin_pb, fin_ma, fin_mb, fin_tp, fin_tm, fin_q,
-    tbuf, zbuf, dbuf, xbuf, dsec_v, qsec_v,
-    own_sem, ds_sem, dr_sem, ss, rs_rly, rs_fin, tsem, zs, zr, ps, pr, xs, xr, small_sem,
+    tbuf, zbuf, zsend, dbuf, xbuf, m_buf, qm_buf, dsec_v, qsec_v,
+    own_sem, ds_sem, dr_sem, ss, rs_rly, rs_fin, tsem, zs, zr, ps, pr, xs, xr, small_sem, hx, hz,
 ):
     dp, tp, cp = lax.axis_index("dp"), lax.axis_index("tensor"), lax.axis_index("ctx")
     y, core = dp // 2, dp % 2
-    nz = zbuf.shape[0]
     cols_all, wide = own_d.shape[1], own_d.shape[2]
     cut = 2 * LANES
     rest = cols_all - cut
@@ -50,6 +50,24 @@
     at = {FAR: (y + 2) % 4, RIGHT: (y + 1) % 4, LEFT: (y + 3) % 4, SELF: y}
     partner = y * 2 + (1 - core)
 
+    def tell(sem, *device):
+        pl.semaphore_signal(sem, inc=1, device_id=device, device_id_type=MESH)
+
+    barrier = pltpu.get_barrier_semaphore()
+    tell(barrier, partner, tp, cp)
+    for k in (1, 3):
+        tell(barrier, ((y + k) % 4) * 2 + core, tp, cp)
+    for k in (1, 3):
+        tell(barrier, dp, (tp + k) % 4, cp)
+
+    @pl.when(cp > 0)
+    def _():
+        tell(barrier, dp, tp, cp - 1)
+
+    @pl.when(cp < nz - 1)
+    def _():
+        tell(barrier, dp, tp, cp + 1)
+
     span = {"A": (0, cut), "B": (cut, rest), "AB": (0, cols_all)}
 
     def main_piece(role, who, part, first, tiles):
@@ -64,8 +82,8 @@
     def query_piece(role, who):
         return gq.at[0, pl.ds(pl.multiple_of((at[role] * 2 + who) * rows_q, 8), rows_q), :]
 
-    order = [("q", FAR), ("t", FAR)] + [("d", FAR, "AB", k, 1) for k in range(TILES)]
-    order += [("q", RIGHT), ("q", LEFT), ("d", RIGHT, "B", 0, TILES), ("t", LEFT), ("d", LEFT, "A", 0, TILES)]
+    order = [("q", FAR), ("q", RIGHT), ("q", LEFT), ("t", FAR)] + [("d", FAR, "AB", k, 1) for k in range(TILES)]
+    order += [("d", RIGHT, "B", 0, TILES), ("t", LEFT), ("d", LEFT, "A", 0, TILES)]
     order += [("t", RIGHT), ("d", RIGHT, "A", 0, TILES), ("d", LEFT, "B", 0, TILES)]
     order += [("q", SELF), ("t", SELF), ("d", SELF, "AB", 0, TILES)]
 
@@ -92,18 +110,7 @@
     for copy in own_copy:
         copy.start()
 
-    barrier = pltpu.get_barrier_semaphore()
-    greeted = 0
-    for k in range(1, 8):
-        pl.semaphore_signal(barrier, inc=1, device_id=((dp + k) % 8, tp, cp), device_id_type=MESH)
-        greeted += 1
-    for k in range(1, 4):
-        pl.semaphore_signal(barrier, inc=1, device_id=(dp, (tp + k) % 4, cp), device_id_type=MESH)
-        greeted += 1
-    for k in (1, nz - 1):
-        pl.semaphore_signal(barrier, inc=1, device_id=(dp, tp, (cp + k) % nz), device_id_type=MESH)
-        greeted += 1
-    pl.semaphore_wait(barrier, greeted)
+    pl.semaphore_wait(barrier, 5 + jnp.where(cp > 0, 1, 0) + jnp.where(cp < nz - 1, 1, 0))
 
     prt_copy = [
         pltpu.make_async_remote_copy(
@@ -115,9 +122,18 @@
     for copy in prt_copy:
         copy.start()
 
+    tell(hx, dp, (tp + 3) % 4, cp)
+
+    @pl.when(jnp.logical_and(cp > 0, cp < nz - 1))
+    def _():
+        tell(hz.at[0], dp, tp, cp - 1)
+        tell(hz.at[1], dp, tp, cp + 1)
+
     small = [
-        pltpu.make_async_copy(dsec, dsec_v, small_sem.at[1]),
-        pltpu.make_async_copy(qsec, qsec_v, small_sem.at[2]),
+        pltpu.make_async_copy(dsec, dsec_v, small_sem.at[0]),
+        pltpu.make_async_copy(qsec, qsec_v, small_sem.at[1]),
+        pltpu.make_async_copy(dm, m_buf, small_sem.at[2]),
+        pltpu.make_async_copy(qm, qm_buf, small_sem.at[3]),
     ]
     for copy in small:
         copy.start()
@@ -209,11 +225,11 @@
         joined[MINUS, k] = store_send(MINUS, value, snd_b.at[2, k], fin_mb.at[k], rs_fin, "f")
 
     first_q()
+    second_q()
     first_t()
     first_d(0)
-    second_q()
+    third_q()
     first_d(1)
-    third_q()
     first_d(2)
     first_d(3)
     second_t()
@@ -223,37 +239,54 @@
     for k in range(TILES):
         third_d(k)
 
+    for copy in small:
+        copy.wait()
+
+    def moment(old, mean):
+        return BETA_ONE * old + (1.0 - BETA_ONE) * mean
+
     head_row = jnp.zeros((1, LANES), F32)
     lane = lax.broadcasted_iota(jnp.int32, (1, LANES), 1)
     for block in (0, 1):
         joined[block, "q"].wait_recv()
         plain[1 - block, "q"].wait_recv()
         mean = (query_sum(SELF, block) + fin_q[block, 1].astype(F32) + fin_q[1 - block, 0].astype(F32)) / 8
-        q_out[:, pl.ds(block * q_half, q_half)] = mean
+        here = (slice(None), pl.ds(block * q_half, q_half))
+        qm_out[here] = moment(qm_buf[here], mean)
         square = jnp.sum(mean * mean, axis=0, keepdims=True)
         for h in range(2):
             part = jnp.sum(square[:, h * LANES:(h + 1) * LANES], axis=1, keepdims=True)
             head_row = jnp.where(lane == block * 2 + h, part, head_row)
-    zbuf[cp] = jnp.broadcast_to(head_row, (8, LANES))
-
-    ring, z_copies = {}, []
-    for s in range(nz // 2):
-        for way, count in ((PLUS, nz // 2), (MINUS, nz - 1 - nz // 2)):
-            if s < count:
-                if s > 0:
-                    ring[way, s - 1].wait_recv()
-                owner = (cp + (nz - s if way == PLUS else s)) % nz
-                ring[way, s] = pltpu.make_async_remote_copy(
-                    src_ref=zbuf.at[owner], dst_ref=zbuf.at[owner],
-                    send_sem=zs.at[way, s], recv_sem=zr.at[way, s],
-                    device_id=(dp, tp, (cp + (1 if way == PLUS else nz - 1)) % nz), device_id_type=MESH)
-                ring[way, s].start()
-                z_copies.append(ring[way, s])
-    ring[PLUS, nz // 2 - 1].wait_recv()
-    ring[MINUS, nz - 2 - nz // 2].wait_recv()
-    head_sum = zbuf[0, pl.ds(0, 1), :]
-    for z in range(1, nz):
-        head_sum = head_sum + zbuf[z, pl.ds(0, 1), :]
+
+    def z_copy(i):
+        step = 1 << i
+        peer = cp + step * (1 - 2 * ((cp // step) % 2))
+        return pltpu.make_async_remote_copy(
+            src_ref=zsend.at[i], dst_ref=zbuf.at[i], send_sem=zs.at[i], recv_sem=zr.at[i],
+            device_id=(dp, tp, peer), device_id_type=MESH)
+
+    @pl.when(cp <= nz - 3)
+    def _():
+        pl.semaphore_wait(hz.at[0], 1)
+
+    @pl.when(cp >= 2)
+    def _():
+        pl.semaphore_wait(hz.at[1], 1)
+
+    @pl.when(jnp.logical_and(cp >= 2, cp <= nz - 3))
+    def _():
+        tell(hz.at[2], dp, tp, cp - 2)
+        tell(hz.at[2], dp, tp, cp + 2)
+
+    z_copies = [z_copy(i) for i in range(3)]
+    zsend[0] = jnp.broadcast_to(head_row, (8, LANES))
+    z_copies[0].start()
+    for i in (1, 2):
+        z_copies[i - 1].wait_recv()
+        zsend[i] = zsend[i - 1] + zbuf[i - 1]
+        if i == 2:
+            pl.semaphore_wait(hz.at[2], 1)
+        z_copies[i].start()
 
     joined["t"].wait_recv()
     plain["t"].wait_recv()
@@ -273,21 +306,26 @@
             swap.wait_recv()
             both = jnp.transpose(tbuf[...])
             own_rows = jnp.where(core == 0, both[:LANES // 2], both[LANES // 2:])
-            t_out[...] = own_rows
+            there = pl.ds(pl.multiple_of((1 - core) * wide, LANES // 2), LANES // 2)
+            m_out[there, :] = moment(m_buf[there, :], own_rows)
             sums_a = sums_a + column_squares(own_rows[:, :cut])
             sums_b = sums_b + column_squares(own_rows[:, cut:])
         plain[MINUS, k].wait_recv()
         joined[PLUS, k].wait_recv()
         mean = (main_sum(SELF, "A", k) + fin_pa[k].astype(F32) + fin_ma[k].astype(F32)) / 8
         rows = jnp.transpose(mean)
-        g_out[k, :, pl.ds(0, cut)] = rows
+        here = pl.ds(pl.multiple_of(core * (LANES // 2) + k * LANES, LANES // 2), LANES)
+        m_out[here, pl.ds(0, cut)] = moment(m_buf[here, pl.ds(0, cut)], rows)
         sums_a = sums_a + column_squares(rows)
         plain[PLUS, k].wait_recv()
         joined[MINUS, k].wait_recv()
         mean = (main_sum(SELF, "B", k) + fin_mb[k].astype(F32) + fin_pb[k].astype(F32)) / 8
         rows = jnp.transpose(mean)
-        g_out[k, :, pl.ds(cut, rest)] = rows
+        m_out[here, pl.ds(cut, rest)] = moment(m_buf[here, pl.ds(cut, rest)], rows)
         sums_b = sums_b + column_squares(rows)
+
+    z_copies[2].wait_recv()
+    head_sum = zsend[2, pl.ds(0, 1), :] + zbuf[2, pl.ds(0, 1), :]
 
     dbuf[dp] = jnp.zeros((8, LANES), F32)
     dbuf[dp, pl.ds(0, 1), :] = sums_a[:, :LANES]
@@ -315,14 +353,13 @@
             total = total + buf[p]
         return total, sends
 
-    for copy in small:
-        copy.wait()
     step = jnp.full((1, LANES), steps[0], jnp.int32).astype(F32)
     keep_one = 1.0 - jnp.exp(step * math.log(BETA_ONE))
     keep_two = 1.0 - jnp.exp(step * math.log(BETA_TWO))
 
     part, p_copies = to_all(dbuf, dp, 8, lambda p: (p, tp, cp), ps, pr)
     xbuf[tp] = part
+    pl.semaphore_wait(hx, 1)
     whole, x_copies = to_all(xbuf, tp, 4, lambda t: (dp, t, cp), xs, xr)
 
     def advance(old, mean, n):
@@ -348,13 +385,11 @@
 
 
 def finish(
-    n_in, g_in, t_in, q_in, dp_in, dm_in, qp_in, qm_in,
+    n_in, m_in, qm_in, dp_in, qp_in,
     dp_out, dm_out, ds_out, du_out, qp_out, qm_out, qs_out, qu_out,
-    po_buf, mo_buf, uo_buf, qpo, qmo, quo, out_sem,
+    po_buf, uo_buf, qpo, quo, out_sem,
 ):
-    core = lax.axis_index("dp") % 2
-    width = dp_in.shape[1]
-    half = LANES // 2
+    rows_d, width = dp_in.shape
     stores = []
 
     def store(src, dst):
@@ -362,32 +397,28 @@
         copy.start()
         stores.append(copy)
 
-    def update(param, moment, grad, scale):
-        moment_new = BETA_ONE * moment + (1.0 - BETA_ONE) * grad
-        step = moment_new * scale
+    def update(param, moment, scale):
+        step = moment * scale
         param_new = param - LEARN_RATE * (step + DECAY_RATE * param)
-        return param_new, moment_new, step.astype(BF16)
-
-    def down(grad, first, count):
-        rows = pl.ds(pl.multiple_of(first, half), count)
+        return param_new, step.astype(BF16)
+
+    block = rows_d // 4
+    store(m_in.at[pl.ds(0, 2 * block), :], dm_out.at[pl.ds(0, 2 * block), :])
+    for b in range(4):
+        rows = pl.ds(b * block, block)
         for k in range(5):
             lanes = pl.ds(k * LANES, LANES if k < 4 else width - 4 * LANES)
-            scale = n_in[k:k + 1, :lanes.size]
-            po_buf[rows, lanes], mo_buf[rows, lanes], uo_buf[rows, lanes] = update(
-                dp_in[rows, lanes], dm_in[rows, lanes], grad[:, lanes], scale)
+            po_buf[rows, lanes], uo_buf[rows, lanes] = update(
+                dp_in[rows, lanes], m_in[rows, lanes], n_in[k:k + 1, :lanes.size])
         store(po_buf.at[rows, :], dp_out.at[rows, :])
-        store(mo_buf.at[rows, :], dm_out.at[rows, :])
         store(uo_buf.at[rows, :], du_out.at[rows, :])
-
-    for k in range(TILES):
-        down(g_in.at[k], core * half + k * LANES, LANES)
-    down(t_in, (1 - core) * TILES * LANES, half)
+        if b == 0:
+            store(m_in.at[pl.ds(2 * block, 2 * block), :], dm_out.at[pl.ds(2 * block, 2 * block), :])
+            store(qm_in, qm_out)
     for h in range(4):
         lanes = pl.ds(h * LANES, LANES)
-        qpo[:, lanes], qmo[:, lanes], quo[:, lanes] = update(
-            qp_in[:, lanes], qm_in[:, lanes], q_in[:, lanes], n_in[5:6, h:h + 1])
+        qpo[:, lanes], quo[:, lanes] = update(qp_in[:, lanes], qm_in[:, lanes], n_in[5:6, h:h + 1])
     store(qpo, qp_out)
-    store(qmo, qm_out)
     store(quo, qu_out)
     for k in range(5):
         count = LANES if k < 4 else width - 4 * LANES
@@ -409,17 +440,16 @@
     pieces = 17
     grad_rows = jnp.swapaxes(grad_down, 1, 2)
     in_hbm = lambda x: pltpu.with_memory_space_constraint(x, pltpu.HBM)
-    g, t, q, n = pl.pallas_call(
-        exchange,
+    m, q_m, n = pl.pallas_call(
+        functools.partial(exchange, nz),
         name="exchange",
         out_shape=(
-            jax.ShapeDtypeStruct((TILES, LANES, width), F32),
-            jax.ShapeDtypeStruct((LANES // 2, width), F32),
+            jax.ShapeDtypeStruct((rows_d, width), F32),
             jax.ShapeDtypeStruct((rows_q, q_width), F32),
             jax.ShapeDtypeStruct((16, LANES), F32),
         ),
-        in_specs=[hbm, hbm, pl.BlockSpec(memory_space=pltpu.SMEM), hbm, hbm],
-        out_specs=(vmem,) * 4,
+        in_specs=[hbm, hbm, hbm, hbm, pl.BlockSpec(memory_space=pltpu.SMEM), hbm, hbm],
+        out_specs=(vmem,) * 3,
         scratch_shapes=[
             pltpu.VMEM((4, width, wide), BF16),
             pltpu.VMEM((4, width, wide), BF16),
@@ -443,18 +473,23 @@
             pltpu.VMEM((t_cols, LANES), BF16),
             pltpu.VMEM((2, 2, rows_q, q_half), BF16),
             pltpu.VMEM((width, LANES), F32),
-            pltpu.VMEM((nz, 8, LANES), F32),
+            pltpu.VMEM((3, 8, LANES), F32),
+            pltpu.VMEM((3, 8, LANES), F32),
             pltpu.VMEM((8, 8, LANES), F32),
             pltpu.VMEM((4, 8, LANES), F32),
+            pltpu.VMEM((rows_d, width), F32),
+            pltpu.VMEM((rows_q, q_width), F32),
             pltpu.VMEM((width,), F32),
             pltpu.SMEM((4,), F32),
             dma((pieces,)), dma((pieces,)), dma((pieces,)),
             dma((33,)), dma((11,)), dma((22,)), dma((2,)),
-            dma((2, nz)), dma((2, nz)), dma((8,)), dma((8,)), dma((4,)), dma((4,)), dma((3,)),
+            dma((3,)), dma((3,)), dma((8,)), dma((8,)), dma((4,)), dma((4,)), dma((4,)),
+            pltpu.SemaphoreType.REGULAR, pltpu.SemaphoreType.REGULAR((3,)),
         ],
         compiler_params=pltpu.CompilerParams(
             collective_id=0, has_side_effects=True, vmem_limit_bytes=28 << 20),
-    )(in_hbm(grad_rows), in_hbm(grad_query), step_count, in_hbm(down_second), in_hbm(query_second))
+    )(in_hbm(grad_rows), in_hbm(grad_query), in_hbm(down_moment), in_hbm(query_moment), step_count,
+      in_hbm(down_second), in_hbm(query_second))
 
     return tuple(pl.pallas_call(
         finish,
@@ -469,19 +504,17 @@
             jax.ShapeDtypeStruct((4,), F32),
             jax.ShapeDtypeStruct((rows_q, q_width), BF16),
         ),
-        in_specs=[vmem] * 8,
+        in_specs=[vmem] * 5,
         out_specs=(hbm, hbm, vmem, hbm, hbm, hbm, vmem, hbm),
         scratch_shapes=[
             pltpu.VMEM((rows_d, width), F32),
-            pltpu.VMEM((rows_d, width), F32),
             pltpu.VMEM((rows_d, width), BF16),
             pltpu.VMEM((rows_q, q_width), F32),
-            pltpu.VMEM((rows_q, q_width), F32),
             pltpu.VMEM((rows_q, q_width), BF16),
-            dma((3 * (TILES + 2),)),
+            dma((13,)),
         ],
         compiler_params=pltpu.CompilerParams(vmem_limit_bytes=24 << 20),
-    )(n, g, t, q, down_param, down_moment, query_param, query_moment))
+    )(n, m, q_m, down_param, query_param))
 
 
 def solution(mesh):

time: 48.9 us -> 46 us (0.941)
  the two profiles are of different devices: /device:TPU:1 before, /device:TPU:96 now
where the time goes in v2:
time: 46 us; the launch traced here: 45.9 us
  Pallas kernels  44.6 us (97%)
  between operations  1.32 us (3%)
    pallas_call x1, Pallas kernels, shards(): pl.pallas_call(functools.partial(exchange, nz), name='exchange', out_shap...  41.9 us
    pallas_call x1, Pallas kernels, shards(): pl.pallas_call(finish, name='finish', out_shape=(jax.ShapeDtypeStruct((ro...  2.65 us

profile of v2, /device:TPU:96, one launch (start us, length us, event | category | flops | bytes accessed | tf_op | source)
XLA Modules:
  0.0 45.9 jit_solution(4138392906867793825)
XLA Ops:
  1.3 0.0 copy-start
  1.3 0.0 copy-start.1
  1.3 41.9 %exchange.1 = (f32[576,576]{1,0:T(8,128)S(1)}, f32[72,512]{1,0:T(8,128)S(1)}, f32[16,128]{1,0:T(8,128)S(1)}) custom-call(bf16[1,576,4608]{2,1,0:T(8,128)(2,1)} %bitcast.1, bf16[1,576,512]{2,1,0:T(8,128)(2,1)} %gq.1, f32[576,576]{1,0:T(8,128)} %dm.1, f32[72,512]{1,0:T(8,128)} %qm.1, s32[1]{0:T(128)S(6)} %copy.17.steps, f32[576]{0:T(1024)} %dsec.1, f32[4]{0:T(128)} %qsec.1), custom_call_target="tpu_custom_call" | custom-call | tf_op jit(solution)/shard_map/exchange/pallas_call | solution.py:443
  43.2 0.0 copy-done
  43.3 0.0 copy-done.1
  43.3 2.6 %finish.1 = (f32[576,576]{1,0:T(8,128)}, f32[576,576]{1,0:T(8,128)}, f32[576]{0:T(1024)}, bf16[576,576]{1,0:T(8,128)(2,1)}, f32[72,512]{1,0:T(8,128)}, /*index=5...) custom-call(f32[16,128]{1,0:T(8,128)S(1)} %get-tuple-element.11.n_in, f32[576,576]{1,0:T(8,128)S(1)} %get-tuple-element.12.m_in, ...), custom_call_target="tpu_custom_call" | custom-call | tf_op jit(solution)/shard_map/finish/pallas_call | solution.py:494
Async XLA Ops:
  1.3 42.0 %copy-start = (f32[576,576]{1,0:T(8,128)S(1)}, f32[576,576]{1,0:T(8,128)}, u32[]{:S(2)}) copy-start(f32[576,576]{1,0:T(8,128)} %dp_in.1) | copy-start | bytes 3981316
  1.3 42.0 %copy-start.1 = (f32[72,512]{1,0:T(8,128)S(1)}, f32[72,512]{1,0:T(8,128)}, u32[]{:S(2)}) copy-start(f32[72,512]{1,0:T(8,128)} %qp_in.1) | copy-start | bytes 442372

commit v3 on v2

--- a/solution.py
+++ b/solution.py
@@ -35,8 +35,8 @@
     own_d, prt_d, own_t, prt_t, own_q, prt_q,
     snd_a, snd_b, snd_t, snd_q, rly_a, rly_b, rly_t, rly_q,
     fin_pa, fin_pb, fin_ma, fin_mb, fin_tp, fin_tm, fin_q,
-    tbuf, zbuf, zsend, dbuf, xbuf, m_buf, qm_buf, dsec_v, qsec_v,
-    own_sem, ds_sem, dr_sem, ss, rs_rly, rs_fin, tsem, zs, zr, ps, pr, xs, xr, small_sem, hx, hz,
+    acc, stage_d, stage_t, stage_q, tbuf, zbuf, zsend, dbuf, m_buf, qm_buf, dsec_v, qsec_v,
+    own_sem, ds_sem, dr_sem, ss, rs_rly, rs_fin, tsem, zs, zr, ps, pr, small_sem, stage_sem, hx, hz, rc, ry, rx,
 ):
     dp, tp, cp = lax.axis_index("dp"), lax.axis_index("tensor"), lax.axis_index("ctx")
     y, core = dp // 2, dp % 2
@@ -54,19 +54,35 @@
         pl.semaphore_signal(sem, inc=1, device_id=device, device_id_type=MESH)
 
     barrier = pltpu.get_barrier_semaphore()
-    tell(barrier, partner, tp, cp)
-    for k in (1, 3):
-        tell(barrier, ((y + k) % 4) * 2 + core, tp, cp)
-    for k in (1, 3):
-        tell(barrier, dp, (tp + k) % 4, cp)
-
-    @pl.when(cp > 0)
-    def _():
-        tell(barrier, dp, tp, cp - 1)
+
+    @pl.when(core == 1)
+    def _():
+        tell(barrier, partner, tp, cp)
+
+    @pl.when(y < 3)
+    def _():
+        tell(barrier, dp + 2, tp, cp)
+
+    @pl.when(y == 0)
+    def _():
+        tell(barrier, 6 + core, tp, cp)
+
+    @pl.when(tp < 3)
+    def _():
+        tell(barrier, dp, tp + 1, cp)
+
+    @pl.when(tp == 0)
+    def _():
+        tell(barrier, dp, 3, cp)
 
     @pl.when(cp < nz - 1)
     def _():
         tell(barrier, dp, tp, cp + 1)
+
+    def one_if(test):
+        return jnp.where(test, 1, 0)
+
+    greeted = (1 - core) + one_if(y > 0) + one_if(y == 3) + one_if(tp > 0) + one_if(tp == 3) + one_if(cp > 0)
 
     span = {"A": (0, cut), "B": (cut, rest), "AB": (0, cols_all)}
 
@@ -107,27 +123,61 @@
         pltpu.make_async_copy(piece(item, core), landing(item, own_d, own_t, own_q), own_sem.at[n])
         for n, item in enumerate(order)
     ]
-    for copy in own_copy:
-        copy.start()
-
-    pl.semaphore_wait(barrier, 5 + jnp.where(cp > 0, 1, 0) + jnp.where(cp < nz - 1, 1, 0))
+    held = {("q", FAR): stage_q.at[0], ("q", RIGHT): stage_q.at[1], ("q", LEFT): stage_q.at[2], ("t", FAR): stage_t,
+            ("d", FAR, "AB", 0, 1): stage_d}
+    stage_copy = [
+        pltpu.make_async_copy(piece(item, 1 - core), held[item], stage_sem.at[n])
+        for n, item in enumerate(order[:len(held)])
+    ]
+    for own, stage in zip(own_copy, stage_copy):
+        own.start()
+        stage.start()
+
+    @pl.when(greeted > 0)
+    def _():
+        pl.semaphore_wait(barrier, greeted)
+
+    @pl.when(core == 0)
+    def _():
+        tell(rc, partner, tp, cp)
+
+    @pl.when(y > 0)
+    def _():
+        tell(ry.at[0], dp - 2, tp, cp)
+
+    @pl.when(y == 3)
+    def _():
+        tell(ry.at[1], core, tp, cp)
+
+    @pl.when(tp > 0)
+    def _():
+        tell(rx.at[0], dp, tp - 1, cp)
+
+    @pl.when(tp == 3)
+    def _():
+        tell(rx.at[1], dp, 0, cp)
+
+    @pl.when(cp > 0)
+    def _():
+        tell(hz.at[3], dp, tp, cp - 1)
+
+    @pl.when(core == 1)
+    def _():
+        pl.semaphore_wait(rc, 1)
 
     prt_copy = [
         pltpu.make_async_remote_copy(
-            src_ref=piece(item, 1 - core), dst_ref=landing(item, prt_d, prt_t, prt_q),
+            src_ref=held.get(item, piece(item, 1 - core)), dst_ref=landing(item, prt_d, prt_t, prt_q),
             send_sem=ds_sem.at[n], recv_sem=dr_sem.at[n],
             device_id=(partner, tp, cp), device_id_type=MESH)
         for n, item in enumerate(order)
     ]
-    for copy in prt_copy:
-        copy.start()
-
-    tell(hx, dp, (tp + 3) % 4, cp)
-
-    @pl.when(jnp.logical_and(cp > 0, cp < nz - 1))
-    def _():
-        tell(hz.at[0], dp, tp, cp - 1)
-        tell(hz.at[1], dp, tp, cp + 1)
+    for n in range(len(stage_copy)):
+        stage_copy[n].wait()
+        prt_copy[n].start()
+    for n in range(len(stage_copy), len(order)):
+        own_copy[n].start()
+        prt_copy[n].start()
 
     small = [
         pltpu.make_async_copy(dsec, dsec_v, small_sem.at[0]),
@@ -185,6 +235,10 @@
 
     def first_q():
         for way in (PLUS, MINUS):
+            @pl.when(y < 3 if way == PLUS else y == 0)
+            def _():
+                pl.semaphore_wait(ry.at[way], 1)
+
             relayed[way, "q"] = store_send(way, query_sum(FAR, way), snd_q.at[way, 0], rly_q.at[way], rs_rly, "r")
 
     def second_q():
@@ -236,8 +290,15 @@
     for k in range(TILES):
         second_d(k)
     third_t()
-    for k in range(TILES):
-        third_d(k)
+
+    @pl.when(cp < nz - 1)
+    def _():
+        pl.semaphore_wait(hz.at[3], 1)
+
+    @pl.when(jnp.logical_and(cp > 0, cp < nz - 1))
+    def _():
+        tell(hz.at[0], dp, tp, cp - 1)
+        tell(hz.at[1], dp, tp, cp + 1)
 
     for copy in small:
         copy.wait()
@@ -265,28 +326,50 @@
             src_ref=zsend.at[i], dst_ref=zbuf.at[i], send_sem=zs.at[i], recv_sem=zr.at[i],
             device_id=(dp, tp, peer), device_id_type=MESH)
 
-    @pl.when(cp <= nz - 3)
-    def _():
-        pl.semaphore_wait(hz.at[0], 1)
-
-    @pl.when(cp >= 2)
-    def _():
-        pl.semaphore_wait(hz.at[1], 1)
-
-    @pl.when(jnp.logical_and(cp >= 2, cp <= nz - 3))
-    def _():
-        tell(hz.at[2], dp, tp, cp - 2)
-        tell(hz.at[2], dp, tp, cp + 2)
-
     z_copies = [z_copy(i) for i in range(3)]
     zsend[0] = jnp.broadcast_to(head_row, (8, LANES))
     z_copies[0].start()
-    for i in (1, 2):
-        z_copies[i - 1].wait_recv()
-        zsend[i] = zsend[i - 1] + zbuf[i - 1]
-        if i == 2:
-            pl.semaphore_wait(hz.at[2], 1)
-        z_copies[i].start()
+
+    @pl.when(cp <= nz - 3)
+    def _():
+        pl.semaphore_wait(hz.at[0], 1)
+
+    @pl.when(cp >= 2)
+    def _():
+        pl.semaphore_wait(hz.at[1], 1)
+
+    @pl.when(jnp.logical_and(cp >= 2, cp <= nz - 3))
+    def _():
+        tell(hz.at[2], dp, tp, cp - 2)
+        tell(hz.at[2], dp, tp, cp + 2)
+
+    for k in range(TILES):
+        third_d(k)
+        if k % 2 == 1:
+            i = (k + 1) // 2
+            z_copies[i - 1].wait_recv()
+            zsend[i] = zsend[i - 1] + zbuf[i - 1]
+            if i == 2:
+                pl.semaphore_wait(hz.at[2], 1)
+            z_copies[i].start()
+
+    sent = 0
+
+    def finish_sends(upto):
+        nonlocal sent
+        for copy in y_copies[sent:upto]:
+            copy.wait_send()
+        sent = upto
+
+    for k in range(TILES):
+        plain[MINUS, k].wait_recv()
+        acc[k, pl.ds(0, cut), :] = main_sum(SELF, "A", k) + fin_ma[k].astype(F32)
+        plain[PLUS, k].wait_recv()
+        acc[k, pl.ds(cut, rest), :] = main_sum(SELF, "B", k) + fin_pb[k].astype(F32)
+
+    for copy in prt_copy + z_copies[:2]:
+        copy.wait_send()
+    finish_sends(len(y_copies) - 1 - 2 * TILES)
 
     joined["t"].wait_recv()
     plain["t"].wait_recv()
@@ -297,12 +380,26 @@
         device_id=(partner, tp, cp), device_id_type=MESH)
     swap.start()
 
+    @pl.when(tp < 3)
+    def _():
+        pl.semaphore_wait(rx.at[0], 1)
+
+    @pl.when(tp == 0)
+    def _():
+        pl.semaphore_wait(rx.at[1], 1)
+
+    tell(hx.at[0], dp, (tp + 3) % 4, cp)
+    tell(hx.at[1], dp, (tp + 1) % 4, cp)
+
     def column_squares(rows):
         return jnp.sum(rows * rows, axis=0, keepdims=True)
 
     sums_a, sums_b = jnp.zeros((1, cut), F32), jnp.zeros((1, rest), F32)
     for k in range(TILES):
         if k == 1:
+            pl.semaphore_wait(hx.at[0], 1)
+            pl.semaphore_wait(hx.at[1], 1)
+            tell(hx.at[2], dp, (tp + 1) % 4, cp)
             swap.wait_recv()
             both = jnp.transpose(tbuf[...])
             own_rows = jnp.where(core == 0, both[:LANES // 2], both[LANES // 2:])
@@ -310,64 +407,71 @@
             m_out[there, :] = moment(m_buf[there, :], own_rows)
             sums_a = sums_a + column_squares(own_rows[:, :cut])
             sums_b = sums_b + column_squares(own_rows[:, cut:])
-        plain[MINUS, k].wait_recv()
+        here = pl.ds(pl.multiple_of(core * (LANES // 2) + k * LANES, LANES // 2), LANES)
         joined[PLUS, k].wait_recv()
-        mean = (main_sum(SELF, "A", k) + fin_pa[k].astype(F32) + fin_ma[k].astype(F32)) / 8
-        rows = jnp.transpose(mean)
-        here = pl.ds(pl.multiple_of(core * (LANES // 2) + k * LANES, LANES // 2), LANES)
-        m_out[here, pl.ds(0, cut)] = moment(m_buf[here, pl.ds(0, cut)], rows)
-        sums_a = sums_a + column_squares(rows)
-        plain[PLUS, k].wait_recv()
+        rows_a = jnp.transpose((acc[k, pl.ds(0, cut), :] + fin_pa[k].astype(F32)) / 8)
         joined[MINUS, k].wait_recv()
-        mean = (main_sum(SELF, "B", k) + fin_mb[k].astype(F32) + fin_pb[k].astype(F32)) / 8
-        rows = jnp.transpose(mean)
-        m_out[here, pl.ds(cut, rest)] = moment(m_buf[here, pl.ds(cut, rest)], rows)
-        sums_b = sums_b + column_squares(rows)
+        rows_b = jnp.transpose((acc[k, pl.ds(cut, rest), :] + fin_mb[k].astype(F32)) / 8)
+        sums_a = sums_a + column_squares(rows_a)
+        sums_b = sums_b + column_squares(rows_b)
+        finish_sends(len(y_copies) - 2 * (TILES - k))
+        if k < TILES - 1:
+            m_out[here, pl.ds(0, cut)] = moment(m_buf[here, pl.ds(0, cut)], rows_a)
+            m_out[here, pl.ds(cut, rest)] = moment(m_buf[here, pl.ds(cut, rest)], rows_b)
+        else:
+            m_out[here, pl.ds(0, cut)] = rows_a
+            m_out[here, pl.ds(cut, rest)] = rows_b
 
     z_copies[2].wait_recv()
     head_sum = zsend[2, pl.ds(0, 1), :] + zbuf[2, pl.ds(0, 1), :]
 
-    dbuf[dp] = jnp.zeros((8, LANES), F32)
-    dbuf[dp, pl.ds(0, 1), :] = sums_a[:, :LANES]
-    dbuf[dp, pl.ds(1, 1), :] = sums_a[:, LANES:]
-    dbuf[dp, pl.ds(2, 1), :] = sums_b[:, :LANES]
-    dbuf[dp, pl.ds(3, 1), :] = sums_b[:, LANES:2 * LANES]
-    dbuf[dp, pl.ds(4, 1), pl.ds(0, LANES // 2)] = sums_b[:, 2 * LANES:]
-    dbuf[dp, pl.ds(5, 1), :] = head_sum
-
-    def to_all(buf, me, size, device, send, recv):
-        sends = []
-        for k in range(1, size):
-            copy = pltpu.make_async_remote_copy(
-                src_ref=buf.at[me], dst_ref=buf.at[me], send_sem=send.at[k], recv_sem=recv.at[me],
-                device_id=device((me + k) % size), device_id_type=MESH)
-            copy.start()
-            sends.append(copy)
-        for k in range(1, size):
-            other = (me + k) % size
-            pltpu.make_async_remote_copy(
-                src_ref=buf.at[other], dst_ref=buf.at[other], send_sem=send.at[k], recv_sem=recv.at[other],
-                device_id=device(other), device_id_type=MESH).wait_recv()
-        total = buf[0]
-        for p in range(1, size):
-            total = total + buf[p]
-        return total, sends
-
+    mine = dbuf.at[tp, dp]
+    mine[pl.ds(0, 1), :] = sums_a[:, :LANES]
+    mine[pl.ds(1, 1), :] = sums_a[:, LANES:]
+    mine[pl.ds(2, 1), :] = sums_b[:, :LANES]
+    mine[pl.ds(3, 1), :] = sums_b[:, LANES:2 * LANES]
+    mine[pl.ds(4, 1), :] = jnp.concatenate([sums_b[:, 2 * LANES:], head_sum[:, :LANES // 2]], axis=1)
+    pl.semaphore_wait(hx.at[2], 1)
+
+    others = [(k, j) for k in (2, 1, 3, 0) for j in (4, 5, 2, 3, 6, 7, 1, 0) if (k, j) != (0, 0)]
+
+    def sums_copy(n, column, row):
+        return pltpu.make_async_remote_copy(
+            src_ref=dbuf.at[column, row], dst_ref=dbuf.at[column, row], send_sem=ps.at[n], recv_sem=pr.at[column, row],
+            device_id=((dp + others[n][1]) % 8, (tp + others[n][0]) % 4, cp), device_id_type=MESH)
+
+    for n in range(len(others)):
+        sums_copy(n, tp, dp).start()
+
+    here = pl.ds(pl.multiple_of(core * (LANES // 2) + (TILES - 1) * LANES, LANES // 2), LANES)
+    m_out[here, :] = moment(m_buf[here, :], m_out[here, :])
     step = jnp.full((1, LANES), steps[0], jnp.int32).astype(F32)
     keep_one = 1.0 - jnp.exp(step * math.log(BETA_ONE))
     keep_two = 1.0 - jnp.exp(step * math.log(BETA_TWO))
-
-    part, p_copies = to_all(dbuf, dp, 8, lambda p: (p, tp, cp), ps, pr)
-    xbuf[tp] = part
-    pl.semaphore_wait(hx, 1)
-    whole, x_copies = to_all(xbuf, tp, 4, lambda t: (dp, t, cp), xs, xr)
+    n_out[...] = jnp.zeros(n_out.shape, F32)
+
+    finish_sends(len(y_copies))
+    swap.wait_send()
+    z_copies[2].wait_send()
+    for n in range(len(others)):
+        sums_copy(n, tp, dp).wait_send()
+    for n, (k, j) in reversed(list(enumerate(others))):
+        sums_copy(n, (tp + k) % 4, (dp + j) % 8).wait_recv()
+
+    def total(column):
+        found = dbuf[column, 0]
+        for p in range(1, 8):
+            found = found + dbuf[column, p]
+        return found
+
+    whole = (total(0) + total(1)) + (total(2) + total(3))
+    part = pltpu.roll(total(tp)[4:5, :], LANES // 2, 1)
 
     def advance(old, mean, n):
         new = BETA_TWO * old + (1.0 - BETA_TWO) * mean
         n_out[n:n + 1, :] = 1.0 / (keep_one * (jnp.sqrt(new / keep_two) + EPSILON))
         n_out[n + 8:n + 9, :] = new
 
-    n_out[...] = jnp.zeros(n_out.shape, F32)
     for k in range(5):
         if k < 4:
             old = dsec_v[pl.ds(k * LANES, LANES)].reshape(1, LANES)
@@ -378,10 +482,7 @@
     old = jnp.ones((1, LANES), F32)
     for h in range(4):
         old = jnp.where(lane == h, qsec_v[h], old)
-    advance(old, part[5:6, :] / (D * HEAD_DIM), 5)
-
-    for copy in prt_copy + y_copies + z_copies + [swap] + p_copies + x_copies:
-        copy.wait_send()
+    advance(old, part / (D * HEAD_DIM), 5)
 
 
 def finish(
@@ -472,19 +573,23 @@
             pltpu.VMEM((t_cols, LANES), BF16),
             pltpu.VMEM((t_cols, LANES), BF16),
             pltpu.VMEM((2, 2, rows_q, q_half), BF16),
+            pltpu.VMEM((TILES, width, LANES), F32),
+            pltpu.VMEM((width, LANES), BF16),
+            pltpu.VMEM((t_cols, LANES), BF16),
+            pltpu.VMEM((3, rows_q, q_width), BF16),
             pltpu.VMEM((width, LANES), F32),
             pltpu.VMEM((3, 8, LANES), F32),
             pltpu.VMEM((3, 8, LANES), F32),
-            pltpu.VMEM((8, 8, LANES), F32),
-            pltpu.VMEM((4, 8, LANES), F32),
+            pltpu.VMEM((4, 8, 5, LANES), F32),
             pltpu.VMEM((rows_d, width), F32),
             pltpu.VMEM((rows_q, q_width), F32),
             pltpu.VMEM((width,), F32),
             pltpu.SMEM((4,), F32),
             dma((pieces,)), dma((pieces,)), dma((pieces,)),
             dma((33,)), dma((11,)), dma((22,)), dma((2,)),
-            dma((3,)), dma((3,)), dma((8,)), dma((8,)), dma((4,)), dma((4,)), dma((4,)),
-            pltpu.SemaphoreType.REGULAR, pltpu.SemaphoreType.REGULAR((3,)),
+            dma((3,)), dma((3,)), dma((31,)), dma((4, 8)), dma((4,)), dma((5,)),
+            pltpu.SemaphoreType.REGULAR((3,)), pltpu.SemaphoreType.REGULAR((4,)),
+            pltpu.SemaphoreType.REGULAR, pltpu.SemaphoreType.REGULAR((2,)), pltpu.SemaphoreType.REGULAR((2,)),
         ],
         compiler_params=pltpu.CompilerParams(
             collective_id=0, has_side_effects=True, vmem_limit_bytes=28 << 20),

time: 46 us -> 42.9 us (0.933)
  the two profiles are of different devices: /device:TPU:96 before, /device:TPU:1 now
where the time goes in v3:
time: 42.9 us; the launch traced here: 42.8 us
  Pallas kernels  41.5 us (97%)
  between operations  1.32 us (3%)
    pallas_call x1, Pallas kernels, shards(): pl.pallas_call(functools.partial(exchange, nz), name='exchange', out_shap...  38.8 us
    pallas_call x1, Pallas kernels, shards(): pl.pallas_call(finish, name='finish', out_shape=(jax.ShapeDtypeStruct((ro...  2.65 us

profile of v3, /device:TPU:1, one launch (start us, length us, event | category | flops | bytes accessed | tf_op | source)
XLA Modules:
  0.0 42.8 jit_solution(13341041014122157138)
XLA Ops:
  1.3 0.0 copy-start
  1.3 0.0 copy-start.1
  1.3 38.8 %exchange.1 = (f32[576,576]{1,0:T(8,128)S(1)}, f32[72,512]{1,0:T(8,128)S(1)}, f32[16,128]{1,0:T(8,128)S(1)}) custom-call(bf16[1,576,4608]{2,1,0:T(8,128)(2,1)} %bitcast.1, bf16[1,576,512]{2,1,0:T(8,128)(2,1)} %gq.1, f32[576,576]{1,0:T(8,128)} %dm.1, f32[72,512]{1,0:T(8,128)} %qm.1, s32[1]{0:T(128)S(6)} %copy.17.steps, f32[576]{0:T(1024)} %dsec.1, f32[4]{0:T(128)} %qsec.1), custom_call_target="tpu_custom_call" | custom-call | tf_op jit(solution)/shard_map/exchange/pallas_call | solution.py:544
  40.1 0.0 copy-done
  40.1 0.0 copy-done.1
  40.1 2.6 %finish.1 = (f32[576,576]{1,0:T(8,128)}, f32[576,576]{1,0:T(8,128)}, f32[576]{0:T(1024)}, bf16[576,576]{1,0:T(8,128)(2,1)}, f32[72,512]{1,0:T(8,128)}, /*index=5...) custom-call(f32[16,128]{1,0:T(8,128)S(1)} %get-tuple-element.11.n_in, f32[576,576]{1,0:T(8,128)S(1)} %get-tuple-element.12.m_in, ...), custom_call_target="tpu_custom_call" | custom-call | tf_op jit(solution)/shard_map/finish/pallas_call | solution.py:599
Async XLA Ops:
  1.3 38.8 %copy-start = (f32[576,576]{1,0:T(8,128)S(1)}, f32[576,576]{1,0:T(8,128)}, u32[]{:S(2)}) copy-start(f32[576,576]{1,0:T(8,128)} %dp_in.1) | copy-start | bytes 3981316
  1.3 38.8 %copy-start.1 = (f32[72,512]{1,0:T(8,128)S(1)}, f32[72,512]{1,0:T(8,128)}, u32[]{:S(2)}) copy-start(f32[72,512]{1,0:T(8,128)} %qp_in.1) | copy-start | bytes 442372

commit v4 on v3

v4 whole, which is shorter than its diff:
```python
import functools
import math

import jax
import jax.numpy as jnp
from jax import lax
from jax.experimental import pallas as pl
from jax.experimental.pallas import tpu as pltpu
from jax.sharding import PartitionSpec as P

D = 4608
HEAD_DIM = 128
FF = 18432

BETA_ONE = 0.9
BETA_TWO = 0.95
EPSILON = 1e-08
LEARN_RATE = 0.003
DECAY_RATE = 0.1

MESH = pl.DeviceIdType.MESH
F32 = jnp.float32
BF16 = jnp.bfloat16

FAR, RIGHT, LEFT, SELF = range(4)
PLUS, MINUS = range(2)
LANES = 128
TILES = 4


def exchange(
    nz,
    gd, gq, dm, qm, steps, dsec, qsec,
    m_out, qm_out, n_out,
    own_d, prt_d, own_t, prt_t, own_q, prt_q,
    snd_a, snd_b, snd_t, snd_q, rly_a, rly_b, rly_t, rly_q,
    fin_pa, fin_pb, fin_ma, fin_mb, fin_t, fin_q,
    acc, stage_d, stage_t, stage_q, tbuf, zbuf, zsend, dbuf, m_buf, qm_buf, dsec_v, qsec_v,
    own_sem, ds_sem, dr_sem, ss, rly_sem, fin_sem, join_sem, tsem, zs, zr, sums_sem, small_sem, stage_sem,
    hx, hz, rc, ry, rx,
):
    div, rem = lax.div, lax.rem
    dp, tp, cp = lax.axis_index("dp"), lax.axis_index("tensor"), lax.axis_index("ctx")
    y, core = div(dp, 2), rem(dp, 2)
    cols_all, wide = own_d.shape[1], own_d.shape[2]
    cut = 2 * LANES
    rest = cols_all - cut
    t_cols = cols_all // 2
    pair = 2 * wide + LANES
    rows_q, q_cols = own_q.shape[1], own_q.shape[2]
    q_half = q_cols // 2
    at = {FAR: rem(y + 2, 4), RIGHT: rem(y + 1, 4), LEFT: rem(y + 3, 4), SELF: y}
    partner = y * 2 + (1 - core)
    after, before = rem(tp + 1, 4), rem(tp + 3, 4)

    def tell(sem, *device):
        pl.semaphore_signal(sem, inc=1, device_id=device, device_id_type=MESH)

    barrier = pltpu.get_barrier_semaphore()

    @pl.when(core == 1)
    def _():
        tell(barrier, partner, tp, cp)

    @pl.when(y < 3)
    def _():
        tell(barrier, dp + 2, tp, cp)

    @pl.when(y == 0)
    def _():
        tell(barrier, 6 + core, tp, cp)

    @pl.when(tp < 3)
    def _():
        tell(barrier, dp, tp + 1, cp)

    @pl.when(tp == 0)
    def _():
        tell(barrier, dp, 3, cp)

    @pl.when(cp < nz - 1)
    def _():
        tell(barrier, dp, tp, cp + 1)

    def one_if(test):
        return jnp.where(test, 1, 0)

    greeted = (1 - core) + one_if(y > 0) + one_if(y == 3) + one_if(tp > 0) + one_if(tp == 3) + one_if(cp > 0)

    span = {"A": (0, cut), "B": (cut, rest), "AB": (0, cols_all)}

    def main_piece(role, who, part, first, tiles):
        row, count = span[part]
        lanes = pl.multiple_of(at[role] * pair + who * (wide + LANES) + first * LANES, LANES)
        return gd.at[0, pl.ds(row, count), pl.ds(lanes, tiles * LANES)]

    def tile_piece(role, who):
        lanes = pl.multiple_of(at[role] * pair + wide, LANES)
        return gd.at[0, pl.ds(pl.multiple_of(who * t_cols, 16), t_cols), pl.ds(lanes, LANES)]

    def query_piece(role, who):
        return gq.at[0, pl.ds(pl.multiple_of((at[role] * 2 + who) * rows_q, 8), rows_q), :]

    order = [(("q", FAR), 0), (("q", RIGHT), 1), (("q", LEFT), 1), (("t", FAR), 2), (("d", FAR, "AB", 0, 1), 3)]
    order += [(("d", FAR, "AB", k, 1), 3 + k) for k in range(1, TILES)]
    order += [(("q", SELF), 11), (("t", LEFT), 7), (("t", RIGHT), 7), (("t", SELF), 7)]
    order += [(("d", RIGHT, "B", 0, TILES), 8), (("d", LEFT, "A", 0, TILES), 8)]
    order += [(("d", RIGHT, "A", 0, TILES), 9), (("d", LEFT, "B", 0, TILES), 9), (("d", SELF, "AB", 0, TILES), 10)]
    own_order = [(("q", FAR), 0), (("t", FAR), 1), (("d", FAR, "AB", 0, TILES), 2)]
    own_rest = [((kind, role), n) for n, kind in ((3, "q"), (4, "t")) for role in (RIGHT, LEFT, SELF)]
    own_rest += [(("d", role, "AB", 0, TILES), 5) for role in (RIGHT, LEFT, SELF)]

    def piece(item, who):
        if item[0] == "q":
            return query_piece(item[1], who)
        if item[0] == "t":
            return tile_piece(item[1], who)
        return main_piece(item[1], who, *item[2:])

    def landing(item, d, t, q):
        if item[0] == "q":
            return q.at[item[1]]
        if item[0] == "t":
            return t.at[item[1]]
        _, role, part, first, tiles = item
        row, count = span[part]
        return d.at[role, pl.ds(row, count), pl.ds(first * LANES, tiles * LANES)]

    def own_load(item, n):
        pltpu.make_async_copy(piece(item, core), landing(item, own_d, own_t, own_q), own_sem.at[n]).start()

    held = {("q", FAR): (stage_q.at[0], 0), ("q", RIGHT): (stage_q.at[1], 1), ("q", LEFT): (stage_q.at[2], 1),
            ("t", FAR): (stage_t, 2), ("d", FAR, "AB", 0, 1): (stage_d, 3)}

    def stage_load(item):
        pltpu.make_async_copy(piece(item, 1 - core), held[item][0], stage_sem.at[held[item][1]]).start()

    stage_load(("q", FAR))
    own_load(*own_order[0])
    stage_load(("q", RIGHT))
    stage_load(("q", LEFT))
    stage_load(("t", FAR))
    own_load(*own_order[1])
    stage_load(("d", FAR, "AB", 0, 1))
    own_load(*own_order[2])
    for entry in own_rest[:3]:
        own_load(*entry)

    @pl.when(greeted > 0)
    def _():
        pl.semaphore_wait(barrier, greeted)

    @pl.when(core == 0)
    def _():
        tell(rc, partner, tp, cp)

    @pl.when(y > 0)
    def _():
        tell(ry.at[0], dp - 2, tp, cp)

    @pl.when(y == 3)
    def _():
        tell(ry.at[1], core, tp, cp)

    @pl.when(tp > 0)
    def _():
        tell(rx.at[0], dp, tp - 1, cp)

    @pl.when(tp == 3)
    def _():
        tell(rx.at[1], dp, 0, cp)

    @pl.when(cp > 0)
    def _():
        tell(hz.at[3], dp, tp, cp - 1)

    @pl.when(core == 1)
    def _():
        pl.semaphore_wait(rc, 1)

    kinds = {"q": 0, "t": 1, "d": 2}
    def settled(ref, sem):
        return pltpu.make_async_remote_copy(
            src_ref=ref, dst_ref=ref, send_sem=sem, recv_sem=sem, device_id=(partner, tp, cp), device_id_type=MESH)

    def prt_start(item, n):
        pltpu.make_async_remote_copy(
            src_ref=held[item][0] if item in held else piece(item, 1 - core), dst_ref=landing(item, prt_d, prt_t, prt_q),
            send_sem=ds_sem.at[kinds[item[0]]], recv_sem=dr_sem.at[n],
            device_id=(partner, tp, cp), device_id_type=MESH).start()

    for n, item in enumerate(list(held)):
        if n != 2:
            ref = stage_q.at[pl.ds(1, 2)] if n == 1 else held[item][0]
            pltpu.make_async_copy(ref, ref, stage_sem.at[held[item][1]]).wait()
        prt_start(*order[n])
    for entry in own_rest[3:6]:
        own_load(*entry)
    for entry in order[len(held):8]:
        prt_start(*entry)
    for entry in own_rest[6:]:
        own_load(*entry)
    for entry in order[8:]:
        prt_start(*entry)

    small = [
        pltpu.make_async_copy(dsec, dsec_v, small_sem.at[0]),
        pltpu.make_async_copy(qsec, qsec_v, small_sem.at[1]),
        pltpu.make_async_copy(dm, m_buf, small_sem.at[2]),
        pltpu.make_async_copy(qm, qm_buf, small_sem.at[3]),
    ]
    for copy in small:
        copy.start()

    have = set()
    three = pl.ds(RIGHT, 3)
    own_ref = [own_q.at[FAR], own_t.at[FAR], own_d.at[FAR], own_q.at[three], own_t.at[three], own_d.at[three]]
    one_tile = prt_d.at[FAR, :, pl.ds(0, LANES)]
    prt_ref = [prt_q.at[FAR], prt_q.at[pl.ds(RIGHT, 2)], prt_t.at[FAR]] + [one_tile] * 4 + [
        prt_t.at[three], prt_d.at[RIGHT], prt_d.at[RIGHT], prt_d.at[SELF], prt_q.at[SELF]]

    def need(own, prt):
        if ("own", own) not in have:
            have.add(("own", own))
            pltpu.make_async_copy(own_ref[own], own_ref[own], own_sem.at[own]).wait()
        if ("prt", prt) not in have:
            have.add(("prt", prt))
            settled(prt_ref[prt], dr_sem.at[prt]).wait_recv()

    def main_sum(role, part, k):
        if role == FAR:
            need(2, 3 + k)
        elif role == SELF:
            need(5, 10)
        else:
            need(5, 8 if (role == RIGHT) == (part == "B") else 9)
        row, count = span[part]
        where = (role, pl.ds(row, count), pl.ds(k * LANES, LANES))
        return own_d[where].astype(F32) + prt_d[where].astype(F32)

    def tile_sum(role):
        need(1, 2) if role == FAR else need(4, 7)
        return own_t[role].astype(F32) + prt_t[role].astype(F32)

    def query_sum(role, block):
        need(0, 0) if role == FAR else need(3, 11 if role == SELF else 1)
        where = (role, slice(None), pl.ds(block * q_half, q_half))
        return own_q[where].astype(F32) + prt_q[where].astype(F32)

    def y_send(way, value, src, send, dst, recv):
        src[...] = value.astype(BF16)
        pltpu.make_async_remote_copy(
            src_ref=src, dst_ref=dst, send_sem=ss.at[send], recv_sem=recv,
            device_id=((at[RIGHT] if way == PLUS else at[LEFT]) * 2 + core, tp, cp), device_id_type=MESH).start()

    def first_q():
        for way in (PLUS, MINUS):
            @pl.when(y < 3 if way == PLUS else y == 0)
            def _():
                pl.semaphore_wait(ry.at[way], 1)

            y_send(way, query_sum(FAR, way), snd_q.at[way, 0], 3, rly_q.at[way], rly_sem.at[9])

    def second_q():
        for way, role in ((PLUS, RIGHT), (MINUS, LEFT)):
            y_send(way, query_sum(role, 1 - way), snd_q.at[way, 1], 3, fin_q.at[way, 0], fin_sem.at[3])

    def third_q():
        settled(rly_q, rly_sem.at[9]).wait_recv()
        for way, role in ((PLUS, RIGHT), (MINUS, LEFT)):
            y_send(way, query_sum(role, way) + rly_q[way].astype(F32), snd_q.at[way, 2], 3, fin_q.at[way, 1], fin_sem.at[3])

    def first_t():
        y_send(PLUS, tile_sum(FAR), snd_t.at[0], 2, rly_t, rly_sem.at[8])

    def second_t():
        y_send(MINUS, tile_sum(LEFT), snd_t.at[1], 2, fin_t.at[0], fin_sem.at[2])

    def third_t():
        settled(rly_t, rly_sem.at[8]).wait_recv()
        y_send(PLUS, tile_sum(RIGHT) + rly_t[...].astype(F32), snd_t.at[2], 2, fin_t.at[1], fin_sem.at[2])

    def first_d(k):
        y_send(PLUS, main_sum(FAR, "A", k), snd_a.at[0, k], 0, rly_a.at[k], rly_sem.at[k])
        y_send(MINUS, main_sum(FAR, "B", k), snd_b.at[0, k], 1, rly_b.at[k], rly_sem.at[4 + k])

    def second_d(k):
        y_send(PLUS, main_sum(RIGHT, "B", k), snd_b.at[1, k], 1, fin_pb.at[k], fin_sem.at[0])
        y_send(MINUS, main_sum(LEFT, "A", k), snd_a.at[1, k], 0, fin_ma.at[k], fin_sem.at[1])

    def third_d(k):
        settled(rly_a.at[k], rly_sem.at[k]).wait_recv()
        y_send(PLUS, main_sum(RIGHT, "A", k) + rly_a[k].astype(F32), snd_a.at[2, k], 0, fin_pa.at[k], join_sem.at[PLUS, k])
        settled(rly_b.at[k], rly_sem.at[4 + k]).wait_recv()
        y_send(MINUS, main_sum(LEFT, "B", k) + rly_b[k].astype(F32), snd_b.at[2, k], 1, fin_mb.at[k], join_sem.at[MINUS, k])

    first_q()
    second_q()
    first_t()
    first_d(0)
    third_q()
    first_d(1)
    first_d(2)
    first_d(3)
    second_t()
    for k in range(TILES):
        second_d(k)
    third_t()

    @pl.when(cp < nz - 1)
    def _():
        pl.semaphore_wait(hz.at[3], 1)

    @pl.when(jnp.logical_and(cp > 0, cp < nz - 1))
    def _():
        tell(hz.at[0], dp, tp, cp - 1)
        tell(hz.at[1], dp, tp, cp + 1)

    for copy in small:
        copy.wait()

    def moment(old, mean):
        return BETA_ONE * old + (1.0 - BETA_ONE) * mean

    head_row = jnp.zeros((1, LANES), F32)
    lane = lax.broadcasted_iota(jnp.int32, (1, LANES), 1)
    settled(fin_q, fin_sem.at[3]).wait_recv()
    for block in (0, 1):
        mean = (query_sum(SELF, block) + fin_q[block, 1].astype(F32) + fin_q[1 - block, 0].astype(F32)) / 8
        where = (slice(None), pl.ds(block * q_half, q_half))
        qm_out[where] = moment(qm_buf[where], mean)
        square = jnp.sum(mean * mean, axis=0, keepdims=True)
        for h in range(2):
            part = jnp.sum(square[:, h * LANES:(h + 1) * LANES], axis=1, keepdims=True)
            head_row = jnp.where(lane == block * 2 + h, part, head_row)

    def z_copy(i):
        step = 1 << i
        peer = cp + step * (1 - 2 * rem(div(cp, step), 2))
        return pltpu.make_async_remote_copy(
            src_ref=zsend.at[i], dst_ref=zbuf.at[i], send_sem=zs, recv_sem=zr.at[i],
            device_id=(dp, tp, peer), device_id_type=MESH)

    z_copies = [z_copy(i) for i in range(3)]
    zsend[0] = jnp.broadcast_to(head_row, (8, LANES))
    z_copies[0].start()

    @pl.when(cp <= nz - 3)
    def _():
        pl.semaphore_wait(hz.at[0], 1)

    @pl.when(cp >= 2)
    def _():
        pl.semaphore_wait(hz.at[1], 1)

    @pl.when(jnp.logical_and(cp >= 2, cp <= nz - 3))
    def _():
        tell(hz.at[2], dp, tp, cp - 2)
        tell(hz.at[2], dp, tp, cp + 2)

    for k in range(TILES):
        third_d(k)
        if k % 2 == 1:
            i = (k + 1) // 2
            z_copies[i - 1].wait_recv()
            zsend[i] = zsend[i - 1] + zbuf[i - 1]
            if i == 2:
                pl.semaphore_wait(hz.at[2], 1)
            z_copies[i].start()

    settled(fin_ma, fin_sem.at[1]).wait_recv()
    settled(fin_pb, fin_sem.at[0]).wait_recv()
    for k in range(TILES):
        acc[k, pl.ds(0, cut), :] = main_sum(SELF, "A", k) + fin_ma[k].astype(F32)
        acc[k, pl.ds(cut, rest), :] = main_sum(SELF, "B", k) + fin_pb[k].astype(F32)
    for n, ref in enumerate((prt_q, prt_t, prt_d)):
        settled(ref, ds_sem.at[n]).wait_send()

    settled(fin_t, fin_sem.at[2]).wait_recv()
    mine = pl.ds(pl.multiple_of(core * t_cols, 8), t_cols)
    tbuf[mine, :] = (tile_sum(SELF) + fin_t[0].astype(F32) + fin_t[1].astype(F32)) / 8
    swap = pltpu.make_async_remote_copy(
        src_ref=tbuf.at[mine, :], dst_ref=tbuf.at[mine, :], send_sem=tsem.at[0], recv_sem=tsem.at[1],
        device_id=(partner, tp, cp), device_id_type=MESH)
    swap.start()

    @pl.when(tp < 3)
    def _():
        pl.semaphore_wait(rx.at[0], 1)

    @pl.when(tp == 0)
    def _():
        pl.semaphore_wait(rx.at[1], 1)

    tell(hx.at[0], dp, before, cp)
    tell(hx.at[1], dp, after, cp)
    settled(snd_q, ss.at[3]).wait_send()
    settled(snd_t, ss.at[2]).wait_send()

    def column_squares(rows):
        return jnp.sum(rows * rows, axis=0, keepdims=True)

    sums_a, sums_b = jnp.zeros((1, cut), F32), jnp.zeros((1, rest), F32)
    for k in range(TILES):
        if k == 1:
            pl.semaphore_wait(hx.at[0], 1)
            pl.semaphore_wait(hx.at[1], 1)
            tell(hx.at[2], dp, after, cp)
            swap.wait_recv()
            both = jnp.transpose(tbuf[...])
            own_rows = jnp.where(core == 0, both[:LANES // 2], both[LANES // 2:])
            there = pl.ds(pl.multiple_of((1 - core) * wide, LANES // 2), LANES // 2)
            m_out[there, :] = moment(m_buf[there, :], own_rows)
            sums_a = sums_a + column_squares(own_rows[:, :cut])
            sums_b = sums_b + column_squares(own_rows[:, cut:])
        here = pl.ds(pl.multiple_of(core * (LANES // 2) + k * LANES, LANES // 2), LANES)
        settled(fin_pa.at[k], join_sem.at[PLUS, k]).wait_recv()
        rows_a = jnp.transpose((acc[k, pl.ds(0, cut), :] + fin_pa[k].astype(F32)) / 8)
        settled(fin_mb.at[k], join_sem.at[MINUS, k]).wait_recv()
        rows_b = jnp.transpose((acc[k, pl.ds(cut, rest), :] + fin_mb[k].astype(F32)) / 8)
        sums_a = sums_a + column_squares(rows_a)
        sums_b = sums_b + column_squares(rows_b)
        if k < TILES - 1:
            m_out[here, pl.ds(0, cut)] = moment(m_buf[here, pl.ds(0, cut)], rows_a)
            m_out[here, pl.ds(cut, rest)] = moment(m_buf[here, pl.ds(cut, rest)], rows_b)
        else:
            m_out[here, pl.ds(0, cut)] = rows_a
            m_out[here, pl.ds(cut, rest)] = rows_b

    z_copies[2].wait_recv()
    head_sum = zsend[2, pl.ds(0, 1), :] + zbuf[2, pl.ds(0, 1), :]

    slot = tp * 8 + dp
    mine = dbuf.at[slot]
    mine[pl.ds(0, 1), :] = sums_a[:, :LANES]
    mine[pl.ds(1, 1), :] = sums_a[:, LANES:]
    mine[pl.ds(2, 1), :] = sums_b[:, :LANES]
    mine[pl.ds(3, 1), :] = sums_b[:, LANES:2 * LANES]
    mine[pl.ds(4, 1), :] = jnp.concatenate([sums_b[:, 2 * LANES:], head_sum[:, :LANES // 2]], axis=1)
    pl.semaphore_wait(hx.at[2], 1)

    others = [(k, j) for k in (2, 1, 3, 0) for j in (4, 5, 2, 3, 6, 7, 1, 0) if (k, j) != (0, 0)]
    for k, j in others:
        pltpu.make_async_remote_copy(
            src_ref=mine, dst_ref=mine, send_sem=sums_sem.at[0], recv_sem=sums_sem.at[1],
            device_id=(rem(dp + j, 8), rem(tp + k, 4), cp), device_id_type=MESH).start()

    here = pl.ds(pl.multiple_of(core * (LANES // 2) + (TILES - 1) * LANES, LANES // 2), LANES)
    m_out[here, :] = moment(m_buf[here, :], m_out[here, :])
    step = jnp.full((1, LANES), steps[0], jnp.int32).astype(F32)
    keep_one = 1.0 - jnp.exp(step * math.log(BETA_ONE))
    keep_two = 1.0 - jnp.exp(step * math.log(BETA_TWO))
    n_out[...] = jnp.zeros(n_out.shape, F32)

    settled(snd_a, ss.at[0]).wait_send()
    settled(snd_b, ss.at[1]).wait_send()
    swap.wait_send()
    settled(zsend, zs).wait_send()
    everyone_else = dbuf.at[pl.ds(0, len(others))]
    settled(everyone_else, sums_sem.at[0]).wait_send()
    settled(everyone_else, sums_sem.at[1]).wait_recv()

    def total(column):
        found = dbuf[column * 8]
        for p in range(1, 8):
            found = found + dbuf[column * 8 + p]
        return found

    whole = (total(0) + total(1)) + (total(2) + total(3))
    part = pltpu.roll(total(tp)[4:5, :], LANES // 2, 1)

    def advance(old, mean, n):
        new = BETA_TWO * old + (1.0 - BETA_TWO) * mean
        n_out[n:n + 1, :] = 1.0 / (keep_one * (jnp.sqrt(new / keep_two) + EPSILON))
        n_out[n + 8:n + 9, :] = new

    for k in range(5):
        if k < 4:
            old = dsec_v[pl.ds(k * LANES, LANES)].reshape(1, LANES)
        else:
            old = dsec_v[pl.ds(k * LANES, LANES // 2)].reshape(1, LANES // 2)
            old = jnp.concatenate([old, jnp.ones((1, LANES // 2), F32)], axis=1)
        advance(old, whole[k:k + 1, :] / FF, k)
    old = jnp.ones((1, LANES), F32)
    for h in range(4):
        old = jnp.where(lane == h, qsec_v[h], old)
    advance(old, part / (D * HEAD_DIM), 5)


def finish(
    n_in, m_in, qm_in, dp_in, qp_in,
    dp_out, dm_out, ds_out, du_out, qp_out, qm_out, qs_out, qu_out,
    po_buf, uo_buf, qpo, quo, ds_buf, qs_buf, out_sem,
):
    rows_d, width = dp_in.shape

    def store(n, src, dst):
        pltpu.make_async_copy(src, dst, out_sem.at[n]).start()

    def update(param, moment, scale):
        step = moment * scale
        param_new = param - LEARN_RATE * (step + DECAY_RATE * param)
        return param_new, step.astype(BF16)

    block = rows_d // 4
    store(0, m_in, dm_out)
    for k in range(5):
        count = LANES if k < 4 else width - 4 * LANES
        ds_buf[pl.ds(k * LANES, count)] = n_in[8 + k:9 + k, :count].reshape(count)
    qs_buf[...] = n_in[13:14, :4].reshape(4)
    store(1, ds_buf, ds_out)
    store(2, qs_buf, qs_out)
    for b in range(4):
        rows = pl.ds(b * block, block)
        for k in range(5):
            lanes = pl.ds(k * LANES, LANES if k < 4 else width - 4 * LANES)
            po_buf[rows, lanes], uo_buf[rows, lanes] = update(
                dp_in[rows, lanes], m_in[rows, lanes], n_in[k:k + 1, :lanes.size])
        store(3, po_buf.at[rows, :], dp_out.at[rows, :])
        store(4, uo_buf.at[rows, :], du_out.at[rows, :])
        if b == 0:
            store(5, qm_in, qm_out)
    for h in range(4):
        lanes = pl.ds(h * LANES, LANES)
        qpo[:, lanes], quo[:, lanes] = update(qp_in[:, lanes], qm_in[:, lanes], n_in[5:6, h:h + 1])
    store(6, qpo, qp_out)
    store(7, quo, qu_out)
    for n, (src, dst) in enumerate((
            (m_in, dm_out), (ds_buf, ds_out), (qs_buf, qs_out), (po_buf, dp_out), (uo_buf, du_out),
            (qm_in, qm_out), (qpo, qp_out), (quo, qu_out))):
        pltpu.make_async_copy(src, dst, out_sem.at[n]).wait()


def shards(nz, grad_down, grad_query, down_param, down_moment, down_second,
           query_param, query_moment, query_second, step_count):
    rows_d, width = down_param.shape
    rows_q, q_width = query_param.shape
    cut, wide = 2 * LANES, TILES * LANES
    rest, t_cols, q_half = width - cut, width // 2, q_width // 2
    hbm = pl.BlockSpec(memory_space=pltpu.HBM)
    vmem = pl.BlockSpec(memory_space=pltpu.VMEM)
    dma = pltpu.SemaphoreType.DMA
    regular = pltpu.SemaphoreType.REGULAR
    grad_rows = jnp.swapaxes(grad_down, 1, 2)
    in_hbm = lambda x: pltpu.with_memory_space_constraint(x, pltpu.HBM)
    m, q_m, n = pl.pallas_call(
        functools.partial(exchange, nz),
        name="exchange",
        out_shape=(
            jax.ShapeDtypeStruct((rows_d, width), F32),
            jax.ShapeDtypeStruct((rows_q, q_width), F32),
            jax.ShapeDtypeStruct((16, LANES), F32),
        ),
        in_specs=[hbm, hbm, hbm, hbm, pl.BlockSpec(memory_space=pltpu.SMEM), hbm, hbm],
        out_specs=(vmem,) * 3,
        scratch_shapes=[
            pltpu.VMEM((4, width, wide), BF16),
            pltpu.VMEM((4, width, wide), BF16),
            pltpu.VMEM((4, t_cols, LANES), BF16),
            pltpu.VMEM((4, t_cols, LANES), BF16),
            pltpu.VMEM((4, rows_q, q_width), BF16),
            pltpu.VMEM((4, rows_q, q_width), BF16),
            pltpu.VMEM((3, TILES, cut, LANES), BF16),
            pltpu.VMEM((3, TILES, rest, LANES), BF16),
            pltpu.VMEM((3, t_cols, LANES), BF16),
            pltpu.VMEM((2, 3, rows_q, q_half), BF16),
            pltpu.VMEM((TILES, cut, LANES), BF16),
            pltpu.VMEM((TILES, rest, LANES), BF16),
            pltpu.VMEM((t_cols, LANES), BF16),
            pltpu.VMEM((2, rows_q, q_half), BF16),
            pltpu.VMEM((TILES, cut, LANES), BF16),
            pltpu.VMEM((TILES, rest, LANES), BF16),
            pltpu.VMEM((TILES, cut, LANES), BF16),
            pltpu.VMEM((TILES, rest, LANES), BF16),
            pltpu.VMEM((2, t_cols, LANES), BF16),
            pltpu.VMEM((2, 2, rows_q, q_half), BF16),
            pltpu.VMEM((TILES, width, LANES), F32),
            pltpu.VMEM((width, LANES), BF16),
            pltpu.VMEM((t_cols, LANES), BF16),
            pltpu.VMEM((3, rows_q, q_width), BF16),
            pltpu.VMEM((width, LANES), F32),
            pltpu.VMEM((3, 8, LANES), F32),
            pltpu.VMEM((3, 8, LANES), F32),
            pltpu.VMEM((32, 5, LANES), F32),
            pltpu.VMEM((rows_d, width), F32),
            pltpu.VMEM((rows_q, q_width), F32),
            pltpu.VMEM((width,), F32),
            pltpu.SMEM((4,), F32),
            dma((6,)), dma((3,)), dma((12,)), dma((4,)), dma((10,)), dma((4,)), dma((2, TILES)), dma((2,)),
            dma, dma((3,)), dma((2,)), dma((4,)), dma((4,)),
            regular((3,)), regular((4,)), regular, regular((2,)), regular((2,)),
        ],
        compiler_params=pltpu.CompilerParams(
            collective_id=0, has_side_effects=True, vmem_limit_bytes=28 << 20),
    )(in_hbm(grad_rows), in_hbm(grad_query), in_hbm(down_moment), in_hbm(query_moment), step_count,
      in_hbm(down_second), in_hbm(query_second))

    return tuple(pl.pallas_call(
        finish,
        name="finish",
        out_shape=(
            jax.ShapeDtypeStruct((rows_d, width), F32),
            jax.ShapeDtypeStruct((rows_d, width), F32),
            jax.ShapeDtypeStruct((width,), F32),
            jax.ShapeDtypeStruct((rows_d, width), BF16),
            jax.ShapeDtypeStruct((rows_q, q_width), F32),
            jax.ShapeDtypeStruct((rows_q, q_width), F32),
            jax.ShapeDtypeStruct((4,), F32),
            jax.ShapeDtypeStruct((rows_q, q_width), BF16),
        ),
        in_specs=[vmem] * 5,
        out_specs=(hbm,) * 8,
        scratch_shapes=[
            pltpu.VMEM((rows_d, width), F32),
            pltpu.VMEM((rows_d, width), BF16),
            pltpu.VMEM((rows_q, q_width), F32),
            pltpu.VMEM((rows_q, q_width), BF16),
            pltpu.VMEM((width,), F32),
            pltpu.VMEM((4,), F32),
            dma((8,)),
        ],
        compiler_params=pltpu.CompilerParams(vmem_limit_bytes=24 << 20),
    )(n, m, q_m, down_param, query_param))


def solution(mesh):
    in_specs = (
        P("dp", "tensor", "ctx"),
        P("dp", "ctx", "tensor"),
        P(("tensor", "dp"), "ctx"),
        P(("tensor", "dp"), "ctx"),
        P("ctx"),
        P(("ctx", "dp"), "tensor"),
        P(("ctx", "dp"), "tensor"),
        P("tensor"),
        P(),
    )
    out_specs = (
        P(("tensor", "dp"), "ctx"),
        P(("tensor", "dp"), "ctx"),
        P("ctx"),
        P(("tensor", "dp"), "ctx"),
        P(("ctx", "dp"), "tensor"),
        P(("ctx", "dp"), "tensor"),
        P("tensor"),
        P(("ctx", "dp"), "tensor"),
    )
    body = functools.partial(shards, mesh.shape["ctx"])
    return jax.shard_map(body, mesh=mesh, in_specs=in_specs, out_specs=out_specs, check_vma=False)
```

time: 42.9 us -> 41.1 us (0.958)
  Pallas kernels: 41.5 us -> 39.6 us
    pallas_call x1, Pallas kernels: 38.8 us -> 37.6 us  [shards(): pl.pallas_call(functools.partial(exchange, nz), name='exchange', out_shap...]
    pallas_call x1, Pallas kernels: 2.65 us -> 2.02 us  [shards(): pl.pallas_call(finish, name='finish', out_shape=(jax.ShapeDtypeStruct((ro...]
where the time goes in v4:
time: 41.1 us; the launch traced here: 40.9 us
  Pallas kernels  39.6 us (96%)
  between operations  1.32 us (3%)
    pallas_call x1, Pallas kernels, shards(): pl.pallas_call(functools.partial(exchange, nz), name='exchange', out_shap...  37.6 us
    pallas_call x1, Pallas kernels, shards(): pl.pallas_call(finish, name='finish', out_shape=(jax.ShapeDtypeStruct((ro...  2.02 us

profile of v4, /device:TPU:1, one launch (start us, length us, event | category | flops | bytes accessed | tf_op | source)
XLA Modules:
  0.0 40.9 jit_solution(15007195345004032638)
XLA Ops:
  1.3 0.0 copy-start
  1.3 0.0 copy-start.1
  1.3 37.6 %exchange.1 = (f32[576,576]{1,0:T(8,128)S(1)}, f32[72,512]{1,0:T(8,128)S(1)}, f32[16,128]{1,0:T(8,128)S(1)}) custom-call(bf16[1,576,4608]{2,1,0:T(8,128)(2,1)} %bitcast.1, bf16[1,576,512]{2,1,0:T(8,128)(2,1)} %gq.1, f32[576,576]{1,0:T(8,128)} %dm.1, f32[72,512]{1,0:T(8,128)} %qm.1, s32[1]{0:T(128)S(6)} %copy.17.steps, f32[576]{0:T(1024)} %dsec.1, f32[4]{0:T(128)} %qsec.1), custom_call_target="tpu_custom_call" | custom-call | tf_op jit(solution)/shard_map/exchange/pallas_call | solution.py:546
  38.9 0.0 copy-done
  38.9 0.0 copy-done.1
  38.9 2.0 %finish.1 = (f32[576,576]{1,0:T(8,128)}, f32[576,576]{1,0:T(8,128)}, f32[576]{0:T(1024)}, bf16[576,576]{1,0:T(8,128)(2,1)}, f32[72,512]{1,0:T(8,128)}, /*index=5...) custom-call(f32[16,128]{1,0:T(8,128)S(1)} %get-tuple-element.11.n_in, f32[576,576]{1,0:T(8,128)S(1)} %get-tuple-element.12.m_in, ...), custom_call_target="tpu_custom_call" | custom-call | tf_op jit(solution)/shard_map/finish/pallas_call | solution.py:598
Async XLA Ops:
  1.3 37.6 %copy-start = (f32[576,576]{1,0:T(8,128)S(1)}, f32[576,576]{1,0:T(8,128)}, u32[]{:S(2)}) copy-start(f32[576,576]{1,0:T(8,128)} %dp_in.1) | copy-start | bytes 3981316
  1.3 37.6 %copy-start.1 = (f32[72,512]{1,0:T(8,128)S(1)}, f32[72,512]{1,0:T(8,128)}, u32[]{:S(2)}) copy-start(f32[72,512]{1,0:T(8,128)} %qp_in.1) | copy-start | bytes 442372

commit v5 on v4

--- a/solution.py
+++ b/solution.py
@@ -32,12 +32,12 @@
     nz,
     gd, gq, dm, qm, steps, dsec, qsec,
     m_out, qm_out, n_out,
-    own_d, prt_d, own_t, prt_t, own_q, prt_q,
-    snd_a, snd_b, snd_t, snd_q, rly_a, rly_b, rly_t, rly_q,
-    fin_pa, fin_pb, fin_ma, fin_mb, fin_t, fin_q,
-    acc, stage_d, stage_t, stage_q, tbuf, zbuf, zsend, dbuf, m_buf, qm_buf, dsec_v, qsec_v,
+    own_d, prt_d, own_q, prt_q,
+    snd_a, snd_b, snd_q, rly_a, rly_b, rly_q,
+    fin_pa, fin_pb, fin_ma, fin_mb, fin_q,
+    own_e, prt_e, snd_e, rly_e, fin_e, acc, stage_d, stage_q, tbuf, zbuf, zsend, dbuf, m_buf, qm_buf, dsec_v, qsec_v,
     own_sem, ds_sem, dr_sem, ss, rly_sem, fin_sem, join_sem, tsem, zs, zr, sums_sem, small_sem, stage_sem,
-    hx, hz, rc, ry, rx,
+    hx, hz, rc, ry, rx, e_sem,
 ):
     div, rem = lax.div, lax.rem
     dp, tp, cp = lax.axis_index("dp"), lax.axis_index("tensor"), lax.axis_index("ctx")
@@ -45,7 +45,7 @@
     cols_all, wide = own_d.shape[1], own_d.shape[2]
     cut = 2 * LANES
     rest = cols_all - cut
-    t_cols = cols_all // 2
+    extra = pl.ds(0, cols_all)
     pair = 2 * wide + LANES
     rows_q, q_cols = own_q.shape[1], own_q.shape[2]
     q_half = q_cols // 2
@@ -94,43 +94,38 @@
         lanes = pl.multiple_of(at[role] * pair + who * (wide + LANES) + first * LANES, LANES)
         return gd.at[0, pl.ds(row, count), pl.ds(lanes, tiles * LANES)]
 
-    def tile_piece(role, who):
-        lanes = pl.multiple_of(at[role] * pair + wide, LANES)
-        return gd.at[0, pl.ds(pl.multiple_of(who * t_cols, 16), t_cols), pl.ds(lanes, LANES)]
+    def extra_piece(role):
+        return gd.at[0, extra, pl.ds(pl.multiple_of(at[role] * pair + wide, LANES), LANES)]
 
     def query_piece(role, who):
         return gq.at[0, pl.ds(pl.multiple_of((at[role] * 2 + who) * rows_q, 8), rows_q), :]
 
-    order = [(("q", FAR), 0), (("q", RIGHT), 1), (("q", LEFT), 1), (("t", FAR), 2), (("d", FAR, "AB", 0, 1), 3)]
-    order += [(("d", FAR, "AB", k, 1), 3 + k) for k in range(1, TILES)]
-    order += [(("q", SELF), 11), (("t", LEFT), 7), (("t", RIGHT), 7), (("t", SELF), 7)]
-    order += [(("d", RIGHT, "B", 0, TILES), 8), (("d", LEFT, "A", 0, TILES), 8)]
-    order += [(("d", RIGHT, "A", 0, TILES), 9), (("d", LEFT, "B", 0, TILES), 9), (("d", SELF, "AB", 0, TILES), 10)]
-    own_order = [(("q", FAR), 0), (("t", FAR), 1), (("d", FAR, "AB", 0, TILES), 2)]
-    own_rest = [((kind, role), n) for n, kind in ((3, "q"), (4, "t")) for role in (RIGHT, LEFT, SELF)]
-    own_rest += [(("d", role, "AB", 0, TILES), 5) for role in (RIGHT, LEFT, SELF)]
+    order = [(("q", FAR), 0), (("q", RIGHT), 1), (("q", LEFT), 1), (("d", FAR, "AB", 0, 1), 2)]
+    order += [(("d", FAR, "AB", k, 1), 2 + k) for k in range(1, TILES)]
+    order += [(("q", SELF), 9)]
+    order += [(("d", RIGHT, "B", 0, TILES), 6), (("d", LEFT, "A", 0, TILES), 6)]
+    order += [(("d", RIGHT, "A", 0, TILES), 7), (("d", LEFT, "B", 0, TILES), 7), (("d", SELF, "AB", 0, TILES), 8)]
+    own_order = [(("q", FAR), 0), (("d", FAR, "AB", 0, TILES), 1)]
+    own_rest = [(("q", role), 2) for role in (RIGHT, LEFT, SELF)]
+    own_rest += [(("d", role, "AB", 0, TILES), 3) for role in (RIGHT, LEFT, SELF)]
 
     def piece(item, who):
         if item[0] == "q":
             return query_piece(item[1], who)
-        if item[0] == "t":
-            return tile_piece(item[1], who)
         return main_piece(item[1], who, *item[2:])
 
-    def landing(item, d, t, q):
+    def landing(item, d, q):
         if item[0] == "q":
             return q.at[item[1]]
-        if item[0] == "t":
-            return t.at[item[1]]
         _, role, part, first, tiles = item
         row, count = span[part]
         return d.at[role, pl.ds(row, count), pl.ds(first * LANES, tiles * LANES)]
 
     def own_load(item, n):
-        pltpu.make_async_copy(piece(item, core), landing(item, own_d, own_t, own_q), own_sem.at[n]).start()
+        pltpu.make_async_copy(piece(item, core), landing(item, own_d, own_q), own_sem.at[n]).start()
 
     held = {("q", FAR): (stage_q.at[0], 0), ("q", RIGHT): (stage_q.at[1], 1), ("q", LEFT): (stage_q.at[2], 1),
-            ("t", FAR): (stage_t, 2), ("d", FAR, "AB", 0, 1): (stage_d, 3)}
+            ("d", FAR, "AB", 0, 1): (stage_d, 2)}
 
     def stage_load(item):
         pltpu.make_async_copy(piece(item, 1 - core), held[item][0], stage_sem.at[held[item][1]]).start()
@@ -139,13 +134,18 @@
     own_load(*own_order[0])
     stage_load(("q", RIGHT))
     stage_load(("q", LEFT))
-    stage_load(("t", FAR))
+    stage_load(("d", FAR, "AB", 0, 1))
     own_load(*own_order[1])
-    stage_load(("d", FAR, "AB", 0, 1))
-    own_load(*own_order[2])
     for entry in own_rest[:3]:
         own_load(*entry)
 
+    def own_extra(role):
+        pltpu.make_async_copy(extra_piece(role), own_e.at[role], e_sem.at[0 if role == FAR else 1]).start()
+
+    @pl.when(core == 1)
+    def _():
+        own_extra(FAR)
+
     @pl.when(greeted > 0)
     def _():
         pl.semaphore_wait(barrier, greeted)
@@ -178,14 +178,14 @@
     def _():
         pl.semaphore_wait(rc, 1)
 
-    kinds = {"q": 0, "t": 1, "d": 2}
+    kinds = {"q": 0, "d": 1}
     def settled(ref, sem):
         return pltpu.make_async_remote_copy(
             src_ref=ref, dst_ref=ref, send_sem=sem, recv_sem=sem, device_id=(partner, tp, cp), device_id_type=MESH)
 
     def prt_start(item, n):
         pltpu.make_async_remote_copy(
-            src_ref=held[item][0] if item in held else piece(item, 1 - core), dst_ref=landing(item, prt_d, prt_t, prt_q),
+            src_ref=held[item][0] if item in held else piece(item, 1 - core), dst_ref=landing(item, prt_d, prt_q),
             send_sem=ds_sem.at[kinds[item[0]]], recv_sem=dr_sem.at[n],
             device_id=(partner, tp, cp), device_id_type=MESH).start()
 
@@ -194,13 +194,30 @@
             ref = stage_q.at[pl.ds(1, 2)] if n == 1 else held[item][0]
             pltpu.make_async_copy(ref, ref, stage_sem.at[held[item][1]]).wait()
         prt_start(*order[n])
-    for entry in own_rest[3:6]:
+    def prt_extra(role):
+        pltpu.make_async_remote_copy(
+            src_ref=extra_piece(role), dst_ref=prt_e.at[role], send_sem=e_sem.at[2], recv_sem=e_sem.at[3 if role == FAR else 4],
+            device_id=(partner, tp, cp), device_id_type=MESH).start()
+
+    @pl.when(core == 0)
+    def _():
+        prt_extra(FAR)
+
+    for entry in order[len(held):7]:
+        prt_start(*entry)
+    for entry in own_rest[3:]:
         own_load(*entry)
-    for entry in order[len(held):8]:
-        prt_start(*entry)
-    for entry in own_rest[6:]:
-        own_load(*entry)
-    for entry in order[8:]:
+    @pl.when(core == 1)
+    def _():
+        for role in (LEFT, RIGHT, SELF):
+            own_extra(role)
+
+    @pl.when(core == 0)
+    def _():
+        for role in (LEFT, RIGHT, SELF):
+            prt_extra(role)
+
+    for entry in order[7:]:
         prt_start(*entry)
 
     small = [
@@ -214,10 +231,10 @@
 
     have = set()
     three = pl.ds(RIGHT, 3)
-    own_ref = [own_q.at[FAR], own_t.at[FAR], own_d.at[FAR], own_q.at[three], own_t.at[three], own_d.at[three]]
+    own_ref = [own_q.at[FAR], own_d.at[FAR], own_q.at[three], own_d.at[three]]
     one_tile = prt_d.at[FAR, :, pl.ds(0, LANES)]
-    prt_ref = [prt_q.at[FAR], prt_q.at[pl.ds(RIGHT, 2)], prt_t.at[FAR]] + [one_tile] * 4 + [
-        prt_t.at[three], prt_d.at[RIGHT], prt_d.at[RIGHT], prt_d.at[SELF], prt_q.at[SELF]]
+    prt_ref = [prt_q.at[FAR], prt_q.at[pl.ds(RIGHT, 2)]] + [one_tile] * 4 + [
+        prt_d.at[RIGHT], prt_d.at[RIGHT], prt_d.at[SELF], prt_q.at[SELF]]
 
     def need(own, prt):
         if ("own", own) not in have:
@@ -229,21 +246,17 @@
 
     def main_sum(role, part, k):
         if role == FAR:
-            need(2, 3 + k)
+            need(1, 2 + k)
         elif role == SELF:
-            need(5, 10)
+            need(3, 8)
         else:
-            need(5, 8 if (role == RIGHT) == (part == "B") else 9)
+            need(3, 6 if (role == RIGHT) == (part == "B") else 7)
         row, count = span[part]
         where = (role, pl.ds(row, count), pl.ds(k * LANES, LANES))
         return own_d[where].astype(F32) + prt_d[where].astype(F32)
 
-    def tile_sum(role):
-        need(1, 2) if role == FAR else need(4, 7)
-        return own_t[role].astype(F32) + prt_t[role].astype(F32)
-
     def query_sum(role, block):
-        need(0, 0) if role == FAR else need(3, 11 if role == SELF else 1)
+        need(0, 0) if role == FAR else need(2, 9 if role == SELF else 1)
         where = (role, slice(None), pl.ds(block * q_half, q_half))
         return own_q[where].astype(F32) + prt_q[where].astype(F32)
 
@@ -270,15 +283,31 @@
         for way, role in ((PLUS, RIGHT), (MINUS, LEFT)):
             y_send(way, query_sum(role, way) + rly_q[way].astype(F32), snd_q.at[way, 2], 3, fin_q.at[way, 1], fin_sem.at[3])
 
-    def first_t():
-        y_send(PLUS, tile_sum(FAR), snd_t.at[0], 2, rly_t, rly_sem.at[8])
-
-    def second_t():
-        y_send(MINUS, tile_sum(LEFT), snd_t.at[1], 2, fin_t.at[0], fin_sem.at[2])
-
-    def third_t():
-        settled(rly_t, rly_sem.at[8]).wait_recv()
-        y_send(PLUS, tile_sum(RIGHT) + rly_t[...].astype(F32), snd_t.at[2], 2, fin_t.at[1], fin_sem.at[2])
+    def extra_sum(role):
+        return own_e[role].astype(F32) + prt_e[role].astype(F32)
+
+    def extra_need(far):
+        for buf, n in ((own_e, 0), (prt_e, 3)):
+            ref = buf.at[FAR] if far else buf.at[three]
+            settled(ref, e_sem.at[n if far else n + 1]).wait_recv()
+
+    def first_e():
+        @pl.when(core == 1)
+        def _():
+            extra_need(True)
+            y_send(PLUS, extra_sum(FAR), snd_e.at[0], 4, rly_e, e_sem.at[5])
+
+    def second_e():
+        @pl.when(core == 1)
+        def _():
+            extra_need(False)
+            y_send(MINUS, extra_sum(LEFT), snd_e.at[1], 4, fin_e.at[0], e_sem.at[6])
+
+    def third_e():
+        @pl.when(core == 1)
+        def _():
+            settled(rly_e, e_sem.at[5]).wait_recv()
+            y_send(PLUS, extra_sum(RIGHT) + rly_e[...].astype(F32), snd_e.at[2], 4, fin_e.at[1], e_sem.at[6])
 
     def first_d(k):
         y_send(PLUS, main_sum(FAR, "A", k), snd_a.at[0, k], 0, rly_a.at[k], rly_sem.at[k])
@@ -296,16 +325,16 @@
 
     first_q()
     second_q()
-    first_t()
     first_d(0)
     third_q()
+    first_e()
     first_d(1)
     first_d(2)
     first_d(3)
-    second_t()
+    second_e()
     for k in range(TILES):
         second_d(k)
-    third_t()
+    third_e()
 
     @pl.when(cp < nz - 1)
     def _():
@@ -373,16 +402,23 @@
     for k in range(TILES):
         acc[k, pl.ds(0, cut), :] = main_sum(SELF, "A", k) + fin_ma[k].astype(F32)
         acc[k, pl.ds(cut, rest), :] = main_sum(SELF, "B", k) + fin_pb[k].astype(F32)
-    for n, ref in enumerate((prt_q, prt_t, prt_d)):
+    for n, ref in enumerate((prt_q, prt_d)):
         settled(ref, ds_sem.at[n]).wait_send()
 
-    settled(fin_t, fin_sem.at[2]).wait_recv()
-    mine = pl.ds(pl.multiple_of(core * t_cols, 8), t_cols)
-    tbuf[mine, :] = (tile_sum(SELF) + fin_t[0].astype(F32) + fin_t[1].astype(F32)) / 8
-    swap = pltpu.make_async_remote_copy(
-        src_ref=tbuf.at[mine, :], dst_ref=tbuf.at[mine, :], send_sem=tsem.at[0], recv_sem=tsem.at[1],
+    swap_extra = pltpu.make_async_remote_copy(
+        src_ref=tbuf.at[extra, :], dst_ref=tbuf.at[extra, :], send_sem=e_sem.at[7], recv_sem=e_sem.at[8],
         device_id=(partner, tp, cp), device_id_type=MESH)
-    swap.start()
+
+    @pl.when(core == 1)
+    def _():
+        settled(fin_e, e_sem.at[6]).wait_recv()
+        tbuf[extra, :] = (extra_sum(SELF) + fin_e[0].astype(F32) + fin_e[1].astype(F32)) / 8
+        swap_extra.start()
+        settled(snd_e, ss.at[4]).wait_send()
+
+    @pl.when(core == 0)
+    def _():
+        settled(prt_e, e_sem.at[2]).wait_send()
 
     @pl.when(tp < 3)
     def _():
@@ -395,7 +431,6 @@
     tell(hx.at[0], dp, before, cp)
     tell(hx.at[1], dp, after, cp)
     settled(snd_q, ss.at[3]).wait_send()
-    settled(snd_t, ss.at[2]).wait_send()
 
     def column_squares(rows):
         return jnp.sum(rows * rows, axis=0, keepdims=True)
@@ -406,7 +441,10 @@
             pl.semaphore_wait(hx.at[0], 1)
             pl.semaphore_wait(hx.at[1], 1)
             tell(hx.at[2], dp, after, cp)
-            swap.wait_recv()
+            @pl.when(core == 0)
+            def _():
+                swap_extra.wait_recv()
+
             both = jnp.transpose(tbuf[...])
             own_rows = jnp.where(core == 0, both[:LANES // 2], both[LANES // 2:])
             there = pl.ds(pl.multiple_of((1 - core) * wide, LANES // 2), LANES // 2)
@@ -454,7 +492,10 @@
 
     settled(snd_a, ss.at[0]).wait_send()
     settled(snd_b, ss.at[1]).wait_send()
-    swap.wait_send()
+    @pl.when(core == 1)
+    def _():
+        swap_extra.wait_send()
+
     settled(zsend, zs).wait_send()
     everyone_else = dbuf.at[pl.ds(0, len(others))]
     settled(everyone_else, sums_sem.at[0]).wait_send()
@@ -536,7 +577,7 @@
     rows_d, width = down_param.shape
     rows_q, q_width = query_param.shape
     cut, wide = 2 * LANES, TILES * LANES
-    rest, t_cols, q_half = width - cut, width // 2, q_width // 2
+    rest, t_cols, q_half = width - cut, width, q_width // 2
     hbm = pl.BlockSpec(memory_space=pltpu.HBM)
     vmem = pl.BlockSpec(memory_space=pltpu.VMEM)
     dma = pltpu.SemaphoreType.DMA
@@ -556,27 +597,26 @@
         scratch_shapes=[
             pltpu.VMEM((4, width, wide), BF16),
             pltpu.VMEM((4, width, wide), BF16),
-            pltpu.VMEM((4, t_cols, LANES), BF16),
-            pltpu.VMEM((4, t_cols, LANES), BF16),
             pltpu.VMEM((4, rows_q, q_width), BF16),
             pltpu.VMEM((4, rows_q, q_width), BF16),
             pltpu.VMEM((3, TILES, cut, LANES), BF16),
             pltpu.VMEM((3, TILES, rest, LANES), BF16),
-            pltpu.VMEM((3, t_cols, LANES), BF16),
             pltpu.VMEM((2, 3, rows_q, q_half), BF16),
             pltpu.VMEM((TILES, cut, LANES), BF16),
             pltpu.VMEM((TILES, rest, LANES), BF16),
-            pltpu.VMEM((t_cols, LANES), BF16),
             pltpu.VMEM((2, rows_q, q_half), BF16),
             pltpu.VMEM((TILES, cut, LANES), BF16),
             pltpu.VMEM((TILES, rest, LANES), BF16),
             pltpu.VMEM((TILES, cut, LANES), BF16),
             pltpu.VMEM((TILES, rest, LANES), BF16),
+            pltpu.VMEM((2, 2, rows_q, q_half), BF16),
+            pltpu.VMEM((4, t_cols, LANES), BF16),
+            pltpu.VMEM((4, t_cols, LANES), BF16),
+            pltpu.VMEM((3, t_cols, LANES), BF16),
+            pltpu.VMEM((t_cols, LANES), BF16),
             pltpu.VMEM((2, t_cols, LANES), BF16),
-            pltpu.VMEM((2, 2, rows_q, q_half), BF16),
             pltpu.VMEM((TILES, width, LANES), F32),
             pltpu.VMEM((width, LANES), BF16),
-            pltpu.VMEM((t_cols, LANES), BF16),
             pltpu.VMEM((3, rows_q, q_width), BF16),
             pltpu.VMEM((width, LANES), F32),
             pltpu.VMEM((3, 8, LANES), F32),
@@ -586,9 +626,9 @@
             pltpu.VMEM((rows_q, q_width), F32),
             pltpu.VMEM((width,), F32),
             pltpu.SMEM((4,), F32),
-            dma((6,)), dma((3,)), dma((12,)), dma((4,)), dma((10,)), dma((4,)), dma((2, TILES)), dma((2,)),
+            dma((6,)), dma((3,)), dma((12,)), dma((5,)), dma((10,)), dma((4,)), dma((2, TILES)), dma((2,)),
             dma, dma((3,)), dma((2,)), dma((4,)), dma((4,)),
-            regular((3,)), regular((4,)), regular, regular((2,)), regular((2,)),
+            regular((3,)), regular((4,)), regular, regular((2,)), regular((2,)), dma((9,)),
         ],
         compiler_params=pltpu.CompilerParams(
             collective_id=0, has_side_effects=True, vmem_limit_bytes=28 << 20),

time: 41.1 us -> 40.8 us (level)
  no operation moved by 1% of the time
where the time goes in v5:
time: 40.8 us; the launch traced here: 40.7 us
  Pallas kernels  39.3 us (96%)
  between operations  1.32 us (3%)
    pallas_call x1, Pallas kernels, shards(): pl.pallas_call(functools.partial(exchange, nz), name='exchange', out_shap...  37.3 us
    pallas_call x1, Pallas kernels, shards(): pl.pallas_call(finish, name='finish', out_shape=(jax.ShapeDtypeStruct((ro...  2.02 us

profile of v5, /device:TPU:1, one launch (start us, length us, event | category | flops | bytes accessed | tf_op | source)
XLA Modules:
  0.0 40.7 jit_solution(3628970365142737272)
XLA Ops:
  1.3 0.0 copy-start
  1.3 0.0 copy-start.1
  1.3 37.3 %exchange.1 = (f32[576,576]{1,0:T(8,128)S(1)}, f32[72,512]{1,0:T(8,128)S(1)}, f32[16,128]{1,0:T(8,128)S(1)}) custom-call(bf16[1,576,4608]{2,1,0:T(8,128)(2,1)} %bitcast.1, bf16[1,576,512]{2,1,0:T(8,128)(2,1)} %gq.1, f32[576,576]{1,0:T(8,128)} %dm.1, f32[72,512]{1,0:T(8,128)} %qm.1, s32[1]{0:T(128)S(6)} %copy.17.steps, f32[576]{0:T(1024)} %dsec.1, f32[4]{0:T(128)} %qsec.1), custom_call_target="tpu_custom_call" | custom-call | tf_op jit(solution)/shard_map/exchange/pallas_call | solution.py:587
  38.6 0.0 copy-done
  38.6 0.0 copy-done.1
  38.6 2.0 %finish.1 = (f32[576,576]{1,0:T(8,128)}, f32[576,576]{1,0:T(8,128)}, f32[576]{0:T(1024)}, bf16[576,576]{1,0:T(8,128)(2,1)}, f32[72,512]{1,0:T(8,128)}, /*index=5...) custom-call(f32[16,128]{1,0:T(8,128)S(1)} %get-tuple-element.11.n_in, f32[576,576]{1,0:T(8,128)S(1)} %get-tuple-element.12.m_in, ...), custom_call_target="tpu_custom_call" | custom-call | tf_op jit(solution)/shard_map/finish/pallas_call | solution.py:638
Async XLA Ops:
  1.3 37.3 %copy-start = (f32[576,576]{1,0:T(8,128)S(1)}, f32[576,576]{1,0:T(8,128)}, u32[]{:S(2)}) copy-start(f32[576,576]{1,0:T(8,128)} %dp_in.1) | copy-start | bytes 3981316
  1.3 37.3 %copy-start.1 = (f32[72,512]{1,0:T(8,128)S(1)}, f32[72,512]{1,0:T(8,128)}, u32[]{:S(2)}) copy-start(f32[72,512]{1,0:T(8,128)} %qp_in.1) | copy-start | bytes 442372

commit v6 on v5

--- a/solution.py
+++ b/solution.py
@@ -626,8 +626,8 @@
             pltpu.VMEM((rows_q, q_width), F32),
             pltpu.VMEM((width,), F32),
             pltpu.SMEM((4,), F32),
-            dma((6,)), dma((3,)), dma((12,)), dma((5,)), dma((10,)), dma((4,)), dma((2, TILES)), dma((2,)),
-            dma, dma((3,)), dma((2,)), dma((4,)), dma((4,)),
+            dma((4,)), dma((2,)), dma((10,)), dma((5,)), dma((10,)), dma((4,)), dma((2, TILES)), dma((1,)),
+            dma, dma((3,)), dma((2,)), dma((4,)), dma((3,)),
             regular((3,)), regular((4,)), regular, regular((2,)), regular((2,)), dma((9,)),
         ],
         compiler_params=pltpu.CompilerParams(

time: 40.8 us -> 40.7 us (level)
  no operation moved by 1% of the time
where the time goes in v6:
time: 40.7 us; the launch traced here: 40.6 us
  Pallas kernels  39.3 us (97%)
  between operations  1.32 us (3%)
    pallas_call x1, Pallas kernels, shards(): pl.pallas_call(functools.partial(exchange, nz), name='exchange', out_shap...  37.2 us
    pallas_call x1, Pallas kernels, shards(): pl.pallas_call(finish, name='finish', out_shape=(jax.ShapeDtypeStruct((ro...  2.02 us

profile of v6, /device:TPU:1, one launch (start us, length us, event | category | flops | bytes accessed | tf_op | source)
XLA Modules:
  0.0 40.6 jit_solution(13440584771775631479)
XLA Ops:
  1.3 0.0 copy-start
  1.3 0.0 copy-start.1
  1.3 37.2 %exchange.1 = (f32[576,576]{1,0:T(8,128)S(1)}, f32[72,512]{1,0:T(8,128)S(1)}, f32[16,128]{1,0:T(8,128)S(1)}) custom-call(bf16[1,576,4608]{2,1,0:T(8,128)(2,1)} %bitcast.1, bf16[1,576,512]{2,1,0:T(8,128)(2,1)} %gq.1, f32[576,576]{1,0:T(8,128)} %dm.1, f32[72,512]{1,0:T(8,128)} %qm.1, s32[1]{0:T(128)S(6)} %copy.17.steps, f32[576]{0:T(1024)} %dsec.1, f32[4]{0:T(128)} %qsec.1), custom_call_target="tpu_custom_call" | custom-call | tf_op jit(solution)/shard_map/exchange/pallas_call | solution.py:587
  38.5 0.0 copy-done
  38.6 0.0 copy-done.1
  38.6 2.0 %finish.1 = (f32[576,576]{1,0:T(8,128)}, f32[576,576]{1,0:T(8,128)}, f32[576]{0:T(1024)}, bf16[576,576]{1,0:T(8,128)(2,1)}, f32[72,512]{1,0:T(8,128)}, /*index=5...) custom-call(f32[16,128]{1,0:T(8,128)S(1)} %get-tuple-element.11.n_in, f32[576,576]{1,0:T(8,128)S(1)} %get-tuple-element.12.m_in, ...), custom_call_target="tpu_custom_call" | custom-call | tf_op jit(solution)/shard_map/finish/pallas_call | solution.py:638
Async XLA Ops:
  1.3 37.3 %copy-start = (f32[576,576]{1,0:T(8,128)S(1)}, f32[576,576]{1,0:T(8,128)}, u32[]{:S(2)}) copy-start(f32[576,576]{1,0:T(8,128)} %dp_in.1) | copy-start | bytes 3981316
  1.3 37.3 %copy-start.1 = (f32[72,512]{1,0:T(8,128)S(1)}, f32[72,512]{1,0:T(8,128)}, u32[]{:S(2)}) copy-start(f32[72,512]{1,0:T(8,128)} %qp_in.1) | copy-start | bytes 442372
